TPU v7x, 256 devices: a whole 4x4x8 slice. The times are simulated.
256 devices in a mesh: section: 16 (over y, z_lo, core), dp: 4 (over x), mp: 4 (over z_hi).
Axes of the slice: x: 4, y: 4, z: 8 (z_hi: 4, z_lo: 2; z = z_hi * 2 + z_lo), core: 2. Of those that a mesh axis runs over, the one named last changes fastest.
Arguments:
- patches: bfloat16 [32768, 1280], P(('section', 'dp')), may hold values from -6 to 6
- patch_counts: int32 [128], P(('section', 'dp')), may hold values from 8 to 256, as said below
- dest_rows: int32 [8192], P(('section', 'dp')), may hold values from 0 to 32767, as said below
- qkv_weight: bfloat16 [1280, 3, 1280], P(None, None, 'mp'), may hold values from -1 to 1
- out_weight: bfloat16 [1280, 1280], P('mp'), may hold values from -0.15625 to 0.15625
- attn_gain: bfloat16 [1280], replicated, may hold values from 0.25 to 1.75
- merge_gain: bfloat16 [1280], replicated, may hold values from 0.25 to 1.75
- fc1_weight: bfloat16 [5120, 5120], P('mp', ('section', 'dp')), may hold values from -0.078125 to 0.078125
- fc1_bias: bfloat16 [5120], P(('section', 'dp')), may hold values from -3 to 3
- fc2_weight: bfloat16 [5120, 8192], P(('section', 'dp'), 'mp'), may hold values from -0.078125 to 0.078125
- fc2_bias: bfloat16 [8192], P('mp'), may hold values from -3 to 3
- text_embeds: bfloat16 [32768, 8192], P(('section', 'dp'), 'mp'), may hold values from -6 to 6
- section_hidden: bfloat16 [32768, 8192], P(('section', 'dp'), 'mp'), may hold values from -80 to 80
- llm_gain: bfloat16 [8192], P('mp'), may hold values from 0.25 to 1.75
Outputs:
- sequence_embeds: bfloat16 [32768, 8192], P(('section', 'dp'), 'mp')
- layer_inputs: bfloat16 [32768, 8192], P(('section', 'dp'), 'mp')
Inputs may be any that keep to these rules, and one draw needn't show every extreme that they name: `patch_counts`: multiples of 4; a tile's patches fill the first slots of its block. `dest_rows`: all rows differ. Each group's merged slots form runs of 2 consecutive slots (aligned); a run goes to one sequence slice (row // 512, numbered in section-major order), different runs of a group to different slices. Rows of slots that are not live are never written.
All inputs are finite; a program needn't handle non-finite values.
Results may differ from a plain program's by a relative error of at most 0.0055.
Values may be sent and summed in bfloat16 or wider, within the bound.
A program may use at most 128 MiB of HBM per device.

v0:
```python
import jax
import jax.numpy as jnp
from jax import lax
from jax.sharding import PartitionSpec as P

HEAD_DIM = 80
HID = 8192


vit_eps = 1e-06
llm_eps = 1e-06


def gather_turned(arrays, axis, dims):
    turned = [jnp.moveaxis(a, dim, 0) for a, dim in zip(arrays, dims)]
    widths = [t[0].size for t in turned]
    both = jnp.concatenate([t.reshape(-1, w) for t, w in zip(turned, widths)], axis=1)
    out = lax.all_gather(both, axis, axis=0, tiled=True)
    blocks = jnp.split(out, [sum(widths[:k]) for k in range(1, len(widths))], axis=1)
    return tuple(
        (
            jnp.moveaxis(b.reshape(-1, *t.shape[1:]), 0, dim)
            for b, t, dim in zip(blocks, turned, dims)
        )
    )


def joined_along(blocks, dim):
    blocks = jnp.moveaxis(blocks, 0, dim)
    shape = blocks.shape
    return blocks.reshape(*shape[:dim], shape[dim] * shape[dim + 1], *shape[dim + 2 :])


def copy_for_each(value, axis):
    copies = jnp.broadcast_to(value, (lax.axis_size(axis), *value.shape))
    return lax.all_to_all(copies, axis, split_axis=0, concat_axis=0, tiled=True)


def gathered_copies(value, axis, dim):
    return joined_along(copy_for_each(value, axis), dim)


def cut_along(value, dim, devices):
    before, after = (value.shape[:dim], value.shape[dim + 1 :])
    return jnp.moveaxis(value.reshape(*before, devices, -1, *after), dim, 0)


def sent_and_summed(value, axis, dim):
    devices = lax.axis_size(axis)
    blocks = lax.all_to_all(cut_along(value, dim, devices), axis, 0, 0, tiled=True)
    return jnp.sum(blocks.astype(jnp.float32), axis=0)


def from_behind(value, axis, steps):
    count = lax.axis_size(axis)
    first, last = (max(0, -steps), min(count, count - steps))
    return lax.ppermute(value, axis, [(source, source + steps) for source in range(first, last)])


def over_copies(value, axis):
    return copy_for_each(value, axis).sum(axis=0)


def layer_norm(values, gain):
    centred = values.astype(jnp.float32)
    centred = centred - jnp.mean(centred, axis=-1, keepdims=True)
    variance = jnp.mean(centred * centred, axis=-1, keepdims=True)
    return centred * lax.rsqrt(variance + vit_eps) * gain.astype(jnp.float32)


def per_device(
    patches,
    patch_counts,
    dest_rows,
    qkv_weight,
    out_weight,
    attn_gain,
    merge_gain,
    fc1_weight,
    fc1_bias,
    fc2_weight,
    fc2_bias,
    text_embeds,
    section_hidden,
    llm_gain,
):
    width = patches.shape[1]
    tile_total = patch_counts.shape[0]
    block_rows = patches.shape[0] // tile_total
    merged_rows = patches.shape[0] // 4
    local_cols = qkv_weight.shape[2]
    local_heads = local_cols // HEAD_DIM
    feature_cols = text_embeds.shape[1]
    seq_rows = text_embeds.shape[0]
    section_count = lax.axis_size("section")
    group_count = section_count * lax.axis_size("dp")
    run_cap = max(2, merged_rows // group_count)
    run_total = merged_rows // run_cap
    normed_in = layer_norm(patches, attn_gain).astype(jnp.bfloat16)
    projections = jnp.dot(
        normed_in, qkv_weight.reshape(width, 3 * local_cols), preferred_element_type=jnp.float32
    ).astype(jnp.bfloat16)
    projections = projections.reshape(tile_total, block_rows, 3, local_heads, HEAD_DIM)
    query_part = projections[:, :, 0]
    key_part = projections[:, :, 1]
    value_part = projections[:, :, 2]
    scores = jnp.einsum(
        "tqhd,tkhd->thqk", query_part, key_part, preferred_element_type=jnp.float32
    ) * HEAD_DIM ** (-0.5)
    key_live = (
        jnp.arange(block_rows, dtype=jnp.int32)[None, None, None, :]
        < patch_counts[:, None, None, None]
    )
    scores = jnp.where(key_live, scores, -1e30)
    weights = jax.nn.softmax(scores, axis=-1).astype(jnp.bfloat16)
    attended = jnp.einsum(
        "thqk,tkhd->tqhd", weights, value_part, preferred_element_type=jnp.float32
    ).astype(jnp.bfloat16)
    attended = attended.reshape(patches.shape[0], local_cols)
    partial_proj = jnp.dot(attended, out_weight, preferred_element_type=jnp.float32)
    position = lax.axis_index("mp")
    own_patch = lax.dynamic_slice_in_dim(
        patches.reshape(merged_rows, 4, width), position, 1, 1
    ).reshape(merged_rows, width)
    own_proj = lax.psum_scatter(
        partial_proj.reshape(merged_rows, 4, width), "mp", scatter_dimension=1, tiled=True
    ).reshape(merged_rows, width)
    block_out = (own_patch.astype(jnp.float32) + own_proj).astype(jnp.bfloat16)
    merge_part = layer_norm(block_out, merge_gain).astype(jnp.bfloat16)
    first_full, second_full, bias_full = gather_turned(
        (fc1_weight, fc2_weight, fc1_bias), "section", (1, 0, 0)
    )
    first_partial = jnp.dot(
        gathered_copies(merge_part, "dp", 0), first_full, preferred_element_type=jnp.float32
    )
    first_total = lax.psum(first_partial.astype(jnp.bfloat16), "mp").astype(jnp.float32)
    hidden = jax.nn.gelu(first_total + bias_full.astype(jnp.float32), approximate=False).astype(
        jnp.bfloat16
    )
    embed_total = sent_and_summed(
        jnp.dot(hidden, second_full, preferred_element_type=jnp.float32).astype(jnp.bfloat16),
        "dp",
        0,
    )
    image_embeds = (embed_total + fc2_bias.astype(jnp.float32)).astype(jnp.bfloat16)
    slot_in_tile = jnp.arange(merged_rows, dtype=jnp.int32) % (block_rows // 4)
    tile_counts = jnp.repeat(patch_counts, block_rows // 4, total_repeat_length=merged_rows)
    live = slot_in_tile * 4 < tile_counts
    receiver = dest_rows // seq_rows
    run_target = receiver.reshape(run_total, run_cap)[:, 0]
    place = jnp.where(live, dest_rows % seq_rows, seq_rows)
    send_rows = (
        jnp.zeros((group_count, run_cap, feature_cols), jnp.bfloat16)
        .at[run_target]
        .set(image_embeds.reshape(run_total, run_cap, feature_cols))
    )
    send_place = (
        jnp.full((group_count, run_cap), seq_rows, jnp.int32)
        .at[run_target]
        .set(place.reshape(run_total, run_cap))
    )
    got_rows, got_place = (
        lax.all_to_all(send_rows, ("section", "dp"), split_axis=0, concat_axis=0, tiled=True),
        lax.all_to_all(send_place, ("section", "dp"), split_axis=0, concat_axis=0, tiled=True),
    )
    sequence_embeds = text_embeds.at[got_place.reshape(-1)].set(
        got_rows.reshape(-1, feature_cols), mode="drop"
    )
    incoming = from_behind(section_hidden, "section", 1)
    entering = jnp.where(lax.axis_index("section") == 0, sequence_embeds, incoming).astype(
        jnp.float32
    )
    row_total = over_copies(jnp.sum(entering * entering, axis=1), "mp")
    layer_inputs = (
        entering * lax.rsqrt(row_total / HID + llm_eps)[:, None] * llm_gain.astype(jnp.float32)
    ).astype(jnp.bfloat16)
    return (sequence_embeds, layer_inputs)


def solution(mesh):
    in_specs = (
        P(("section", "dp"), None),
        P(("section", "dp")),
        P(("section", "dp")),
        P(None, None, "mp"),
        P("mp", None),
        P(),
        P(),
        P("mp", ("section", "dp")),
        P(("section", "dp")),
        P(("section", "dp"), "mp"),
        P("mp"),
        P(("section", "dp"), "mp"),
        P(("section", "dp"), "mp"),
        P("mp"),
    )
    out_specs = (P(("section", "dp"), "mp"), P(("section", "dp"), "mp"))
    return jax.shard_map(
        per_device, mesh=mesh, in_specs=in_specs, out_specs=out_specs, check_vma=False
    )
```

profile of v0, /device:TPU:8, one launch (start us, length us, event | category | flops | bytes accessed | tf_op | source)
XLA Modules:
  0.0 324.2 jit_solution(17238749150550705226)
XLA Ops:
  8.1 3.3 %copy.101 = bf16[512,2048]{1,0:T(8,128)(2,1)} copy(bf16[512,2048]{1,0:T(8,128)(2,1)} %param.27) | data formatting | bytes 4194304
  12.2 2.6 convolution_convert_fusion
  14.8 2.5 reshape.190
  18.9 3.3 %fusion.122 = (f32[2,4,256]{2,1,0:T(4,128)S(1)}, f32[2,4,256,256]{2,3,1,0:T(8,128)}) fusion(pred[2,256]{1,0:T(4,128)(4,1)S(1)} %iota_compare_fusion, bf16[2,256,1,4,80]{1,0,4,3,2:T(2,128)(2,1)} %get-tuple-element.18, bf16[2,256,1,4,80]{1,0,4,3,2:T(2,128)(2,1)} %get-tuple-element.17), kind=kOutput, calls=%fused_computation.164 | convolution fusion | flops 85983488 | bytes 2761216 | tf_op jit(solution)/shard_map/sub | solution.py:115
  25.0 3.6 %fusion.73 = f32[128,4,1280]{2,0,1:T(8,128)} fusion(bf16[320,1280]{1,0:T(8,128)(2,1)} %param.20, bf16[128,4,320]{2,1,0:T(4,128)(2,1)S(1)} %dot_general.23), kind=kOutput, calls=%fused_computation.91 | convolution fusion | flops 419430400 | bytes 3768320 | tf_op jit(solution)/shard_map/dot_general | solution.py:120
  30.4 3.5 %reshape.188 = bf16[128,4,1280]{2,1,0:T(4,128)(2,1)} reshape(bf16[512,1280]{1,0:T(8,128)(2,1)} %param.16) | data formatting | bytes 2621440 | tf_op jit(solution)/shard_map/reshape | solution.py:123
  35.9 54.7 %reduce-scatter.2.cloned.1.call-done = f32[128,1,1280]{2,0,1:T(8,128)} async-done(((f32[128,4,1280]{2,0,1:T(8,128)}), f32[128,1,1280]{2,0,1:T(8,128)}) %reduce-scatter.2.cloned.1.call-update) | async-done | bytes 655376 | tf_op jit(solution)/shard_map/reduce_scatter | solution.py:125
  92.5 22.0 %all_to_all.30 = bf16[4,128,1280]{2,1,0:T(8,128)(2,1)} all-to-all(bf16[4,128,1280]{2,1,0:T(8,128)(2,1)S(1)} %broadcast_in_dim.30), channel_id=1, replica_groups=mesh['section'=16,'dp'=4,'mp'=4] {'dp'}, dimensions={0} | all-to-all | bytes 2621440 | tf_op jit(solution)/shard_map/all_to_all | solution.py:36
  114.5 13.1 %all-gather.2.cloned.1.call-done = bf16[1280,3329]{1,0:T(8,128)(2,1)} async-done(((bf16[80,3329]{1,0:T(8,128)(2,1)}), bf16[1280,3329]{1,0:T(8,128)(2,1)}) %all-gather.2.cloned.1.call-update) | async-done | bytes 8522256 | tf_op jit(solution)/shard_map/all_gather | solution.py:18
  127.6 5.3 %fusion.10 = bf16[512,1280]{1,0:T(8,128)(2,1)} fusion(bf16[512,1280]{1,0:T(8,128)(2,1)} %bitcast.62, bf16[1280,3329]{1,0:T(8,128)(2,1)} %all-gather.2.cloned.1.call-done), kind=kOutput, calls=%fused_computation.19 | convolution fusion | flops 1678376960 | bytes 5898240 | tf_op jit(solution)/shard_map/dot_general | solution.py:133
  134.0 75.5 %all-reduce.2.cloned.1.call-done = bf16[512,1280]{1,0:T(8,128)(2,1)} async-done(((bf16[512,1280]{1,0:T(8,128)(2,1)}), bf16[512,1280]{1,0:T(8,128)(2,1)}) %all-reduce.2.cloned.1.call-update) | async-done | bytes 1310736 | tf_op jit(solution)/shard_map/psum | solution.py:136
  209.5 12.3 %fusion.13 = bf16[512,2048]{1,0:T(8,128)(2,1)} fusion(bf16[1280,3329]{1,0:T(8,128)(2,1)} %all-gather.2.cloned.1.call-done, bf16[512,1280]{1,0:T(8,128)(2,1)} %all-reduce.2.cloned.1.call-done, f32[1280]{0:T(1024)S(1)} %convert_reduce_fusion.3), kind=kOutput, calls=%fused_computation.20 | convolution fusion | flops 2729312256 | bytes 8655872 | tf_op jit(solution)/shard_map/dot_general | solution.py:141
  221.9 4.6 %all-to-all-start.2 = ((bf16[4,128,2048]{2,1,0:T(8,128)(2,1)}), bf16[4,128,2048]{2,1,0:T(8,128)(2,1)}, u32[]{:S(2)}, u32[]{:S(2)}) async-start(bf16[4,128,2048]{2,1,0:T(8,128)(2,1)} %bitcast.61), calls=%async_computation.3 | async-start | bytes 4194304 | tf_op jit(solution)/shard_map/all_to_all | solution.py:50
  231.9 21.2 %all-to-all-done.2 = bf16[4,128,2048]{2,1,0:T(8,128)(2,1)} async-done(((bf16[4,128,2048]{2,1,0:T(8,128)(2,1)}), bf16[4,128,2048]{2,1,0:T(8,128)(2,1)}, u32[]{:S(2)}, u32[]{:S(2)}) %all-to-all-start.2) | async-done | bytes 2097184 | tf_op jit(solution)/shard_map/all_to_all | solution.py:50
  253.2 6.0 %all-to-all-start = ((s32[64,1,2]{2,1,0:T(1,128)}), s32[64,1,2]{2,1,0:T(1,128)S(1)}, u32[]{:S(2)}, u32[]{:S(2)}) async-start(s32[64,1,2]{2,1,0:T(1,128)} %bitcast.15), calls=%async_computation | async-start | bytes 65536 | tf_op jit(solution)/shard_map/all_to_all | solution.py:164
  259.2 2.1 convert_reduce_fusion
  265.6 8.0 %scatter_fusion = bf16[64,2,2048]{2,1,0:T(2,128)(2,1)} fusion(bf16[64,2,2048]{2,1,0:T(2,128)(2,1)} %broadcast_in_dim.24, s32[64]{0:T(128)S(1)} %fusion.83, bf16[64,2,2048]{2,1,0:T(2,128)(2,1)S(1)} %add_convert_fusion), kind=kCustom, calls=%fused_computation.1 | custom fusion | bytes 1573120 | tf_op jit(solution)/shard_map/scatter | solution.py:155
  273.5 8.8 %all-to-all-start.3 = ((bf16[64,2,2048]{2,1,0:T(2,128)(2,1)}), bf16[64,2,2048]{2,1,0:T(2,128)(2,1)S(1)}, u32[]{:S(2)}, u32[]{:S(2)}) async-start(bf16[64,2,2048]{2,1,0:T(2,128)(2,1)} %scatter_fusion), calls=%async_computation.4 | async-start | bytes 1048576 | tf_op jit(solution)/shard_map/all_to_all | solution.py:163
  283.8 9.5 %all-to-all-done.3 = bf16[64,2,2048]{2,1,0:T(2,128)(2,1)S(1)} async-done(((bf16[64,2,2048]{2,1,0:T(2,128)(2,1)}), bf16[64,2,2048]{2,1,0:T(2,128)(2,1)S(1)}, u32[]{:S(2)}, u32[]{:S(2)}) %all-to-all-start.3) | async-done | bytes 524320 | tf_op jit(solution)/shard_map/all_to_all | solution.py:163
  293.4 4.6 %scatter_fusion.1 = bf16[512,2048]{1,0:T(8,128)(2,1)} fusion(bf16[512,2048]{1,0:T(8,128)(2,1)} %copy.101, s32[128]{0:T(128)S(1)} %fusion.87, bf16[128,2048]{1,0:T(8,128)(2,1)S(1)} %reshape.225), kind=kCustom, calls=%fused_computation.2 | custom fusion | bytes 1573376 | tf_op jit(solution)/shard_map/scatter | solution.py:166
  298.1 2.4 fusion.3
  301.0 3.9 %all-to-all-start.4 = ((f32[4,1,512]{2,1,0:T(1,128)}), f32[4,1,512]{2,1,0:T(1,128)S(1)}, u32[]{:S(2)}, u32[]{:S(2)}) async-start(f32[4,1,512]{2,1,0:T(1,128)} %broadcast_in_dim.31), calls=%async_computation.5 | async-start | bytes 16384 | tf_op jit(solution)/shard_map/all_to_all | solution.py:36
  304.9 7.7 %all-to-all-done.4 = f32[4,1,512]{2,1,0:T(1,128)S(1)} async-done(((f32[4,1,512]{2,1,0:T(1,128)}), f32[4,1,512]{2,1,0:T(1,128)S(1)}, u32[]{:S(2)}, u32[]{:S(2)}) %all-to-all-start.4) | async-done | bytes 8224 | tf_op jit(solution)/shard_map/all_to_all | solution.py:36
  312.6 4.1 %fusion.5 = bf16[512,2048]{1,0:T(8,128)(2,1)} fusion(f32[2048]{0:T(1024)S(1)} %convert_element_type.105, f32[512]{0:T(512)S(1)} %add_rsqrt_fusion, bf16[512,2048]{1,0:T(8,128)(2,1)} %scatter_fusion.1, bf16[512,2048]{1,0:T(8,128)(2,1)} %collective-permute-done, pred[]{:T(512)S(6)} %eq.6), kind=kLoop, calls=%fused_computation.10 | loop fusion | flops 5242880 | bytes 6301697 | tf_op jit(solution)/shard_map/convert_element_type | solution.py:176
  (75 shorter events, 23.9 us)
Async XLA Ops:
  8.0 4.2 %copy-start = (bf16[1280,3,320]{0,2,1:T(8,128)(2,1)S(1)}, bf16[1280,3,320]{0,2,1:T(8,128)(2,1)}, u32[]{:S(2)}) copy-start(bf16[1280,3,320]{0,2,1:T(8,128)(2,1)} %param.19) | copy-start | bytes 7372804
  8.0 4.1 %copy-start.5 = (bf16[1280]{0:T(1024)(128)(2,1)S(1)}, bf16[1280]{0:T(1024)(128)(2,1)}, u32[]{:S(2)}) copy-start(bf16[1280]{0:T(1024)(128)(2,1)} %param.21) | copy-start | bytes 7684
  8.0 82.6 %reduce-scatter.2.cloned.1.call-start = ((), (), s32[]{:S(2)}) async-start(), calls=%async_computation.6 | async-start | bytes 3276800 | tf_op jit(solution)/shard_map/reduce_scatter | solution.py:125
  8.1 3.3 %copy-start.1 = (bf16[512,1280]{1,0:T(8,128)(2,1)S(1)}, bf16[512,1280]{1,0:T(8,128)(2,1)}, u32[]{:S(2)}) copy-start(bf16[512,1280]{1,0:T(8,128)(2,1)} %param.16) | copy-start | bytes 3932164
  14.8 4.1 %copy-start.9 = (s32[2]{0:T(128)S(1)}, s32[2]{0:T(128)}, u32[]{:S(2)}) copy-start(s32[2]{0:T(128)} %param.17) | copy-start | bytes 28
  18.9 3.4 %copy-start.3 = (bf16[2,256,1,4,80]{1,0,4,3,2:T(2,128)(2,1)S(1)}, bf16[2,256,1,4,80]{1,0,4,3,2:T(2,128)(2,1)}, u32[]{:S(2)}) copy-start(bf16[2,256,1,4,80]{1,0,4,3,2:T(2,128)(2,1)} %get-tuple-element.16) | copy-start | bytes 983044
  24.9 3.7 %copy-start.12 = (bf16[80]{0:T(256)(128)(2,1)S(1)}, bf16[80]{0:T(256)(128)(2,1)}, u32[]{:S(2)}) copy-start(bf16[80]{0:T(256)(128)(2,1)} %param.24) | copy-start | bytes 484
  25.0 3.8 %copy-start.2 = (bf16[80,2048]{1,0:T(8,128)(2,1)S(1)}, bf16[80,2048]{1,0:T(8,128)(2,1)}, u32[]{:S(2)}) copy-start(bf16[80,2048]{1,0:T(8,128)(2,1)} %param.25) | copy-start | bytes 983044
  28.6 0.9 copy-start.4
  28.6 5.3 %copy-start.6 = (bf16[1280]{0:T(1024)(128)(2,1)S(1)}, bf16[1280]{0:T(1024)(128)(2,1)}, u32[]{:S(2)}) copy-start(bf16[1280]{0:T(1024)(128)(2,1)} %param.22) | copy-start | bytes 7684
  28.6 99.0 %all-gather.2.cloned.1.call-start = ((), (), s32[]{:S(2)}) async-start(), calls=%async_computation.7 | async-start | bytes 9400320 | tf_op jit(solution)/shard_map/all_gather | solution.py:18
  30.4 179.1 %all-reduce.2.cloned.1.call-start = ((), (), s32[]{:S(2)}) async-start(), calls=%async_computation.8 | async-start | bytes 2621440 | tf_op jit(solution)/shard_map/psum | solution.py:136
  221.9 7.1 %copy-start.7 = (bf16[2048]{0:T(1024)(128)(2,1)S(1)}, bf16[2048]{0:T(1024)(128)(2,1)}, u32[]{:S(2)}) copy-start(bf16[2048]{0:T(1024)(128)(2,1)} %param.26) | copy-start | bytes 12292
  221.9 7.1 %copy-start.10 = (s32[128]{0:T(128)S(1)}, s32[128]{0:T(128)}, u32[]{:S(2)}) copy-start(s32[128]{0:T(128)} %param.18) | copy-start | bytes 1540
  221.9 7.1 %copy-start.11 = (pred[128]{0:T(512)(128)(4,1)S(1)}, pred[128]{0:T(512)(128)(4,1)}, u32[]{:S(2)}) copy-start(pred[128]{0:T(512)(128)(4,1)} %constant.225) | copy-start | bytes 388
  221.9 31.3 %all-to-all-start.2 = ((bf16[4,128,2048]{2,1,0:T(8,128)(2,1)}), bf16[4,128,2048]{2,1,0:T(8,128)(2,1)}, u32[]{:S(2)}, u32[]{:S(2)}) async-start(bf16[4,128,2048]{2,1,0:T(8,128)(2,1)} %bitcast.61), calls=%async_computation.3 | async-start | bytes 4194304 | tf_op jit(solution)/shard_map/all_to_all | solution.py:50
  226.5 71.6 %collective-permute-start = (bf16[512,2048]{1,0:T(8,128)(2,1)}, bf16[512,2048]{1,0:T(8,128)(2,1)}, u32[]{:S(2)}, u32[]{:S(2)}) collective-permute-start(bf16[512,2048]{1,0:T(8,128)(2,1)} %param.28), channel_id=1, source_target_pairs={{0,16},{16,32},{32,48},{48,64},{64,80},{80,96},{96,112},{112,128},... | collective-permute-start | bytes 6291464 | tf_op jit(solution)/shard_map/ppermute | solution.py:57
  253.2 20.4 %all-to-all-start = ((s32[64,1,2]{2,1,0:T(1,128)}), s32[64,1,2]{2,1,0:T(1,128)S(1)}, u32[]{:S(2)}, u32[]{:S(2)}) async-start(s32[64,1,2]{2,1,0:T(1,128)} %bitcast.15), calls=%async_computation | async-start | bytes 65536 | tf_op jit(solution)/shard_map/all_to_all | solution.py:164
  273.5 19.7 %all-to-all-start.3 = ((bf16[64,2,2048]{2,1,0:T(2,128)(2,1)}), bf16[64,2,2048]{2,1,0:T(2,128)(2,1)S(1)}, u32[]{:S(2)}, u32[]{:S(2)}) async-start(bf16[64,2,2048]{2,1,0:T(2,128)(2,1)} %scatter_fusion), calls=%async_computation.4 | async-start | bytes 1048576 | tf_op jit(solution)/shard_map/all_to_all | solution.py:163
  298.1 6.8 %copy-start.8 = (bf16[2048]{0:T(1024)(128)(2,1)S(1)}, bf16[2048]{0:T(1024)(128)(2,1)}, u32[]{:S(2)}) copy-start(bf16[2048]{0:T(1024)(128)(2,1)} %param.29) | copy-start | bytes 12292
  301.0 11.6 %all-to-all-start.4 = ((f32[4,1,512]{2,1,0:T(1,128)}), f32[4,1,512]{2,1,0:T(1,128)S(1)}, u32[]{:S(2)}, u32[]{:S(2)}) async-start(f32[4,1,512]{2,1,0:T(1,128)} %broadcast_in_dim.31), calls=%async_computation.5 | async-start | bytes 16384 | tf_op jit(solution)/shard_map/all_to_all | solution.py:36
Sparse Core Ops, SparseCore 0:
  28.7 61.8 reduce-scatter.1
  133.0 76.4 all-reduce.1
Sparse Core Ops, SparseCore 1:
  30.9 96.6 all-gather.1
where the time goes:
time: 326 us; the launch traced here: 324 us
  waiting for transfers between devices  182 us (56%)
  local copies, waits for them, and re-layouts  33.5 us (10%)
  matrix products  29 us (9%)
  starting transfers between devices  25.3 us (8%)
  blocking collectives  22 us (7%)
  other arithmetic  16.8 us (5%)
  between operations  15.8 us (5%)
    psum x1, waiting for transfers between devices, per_device(): lax.psum(first_partial.astype(jnp.bfloat16), 'mp').astype(jnp.float32)  75.5 us
    reduce_scatter x1, waiting for transfers between devices, per_device(): lax.psum_scatter(partial_proj.reshape(merged_rows, 4, width), 'mp', scatt...  54.7 us
    all_to_all x1, blocking collectives, copy_for_each(): return lax.all_to_all(copies, axis, split_axis=0, concat_axis=0, tiled=True)  22 us
    all_to_all x1, waiting for transfers between devices, sent_and_summed(): lax.all_to_all(cut_along(value, dim, devices), axis, 0, 0, tiled=True)  21.2 us
    all_gather x1, waiting for transfers between devices, gather_turned(): out = lax.all_gather(both, axis, axis=0, tiled=True)  13.1 us
    dot_general x1, matrix products, per_device(): jnp.dot(hidden, second_full, preferred_element_type=jnp.float32)  12.3 us
    all_to_all x1, waiting for transfers between devices, per_device(): lax.all_to_all(send_rows, ('section', 'dp'), split_axis=0, concat_axis=0,...  9.47 us
    all_to_all x1, starting transfers between devices, per_device(): lax.all_to_all(send_rows, ('section', 'dp'), split_axis=0, concat_axis=0,...  8.83 us
  transfers between devices with their start and end apart: 8, of which 6 were waited for; matrix products, arithmetic and copies ran while one was open for 10% of the time, Pallas kernels for 0%

commit v1 on v0

v1 whole, which is shorter than its diff:
```python
import jax
import jax.numpy as jnp
from jax import lax
from jax.experimental import pallas as pl
from jax.experimental.pallas import tpu as pltpu
from jax.sharding import PartitionSpec as P

HEAD_DIM = 80
HID = 8192
MESH = pl.DeviceIdType.MESH
BF = jnp.bfloat16
F32 = jnp.float32

vit_eps = 1e-06
llm_eps = 1e-06


def place():
    s = lax.axis_index("section")
    x = lax.axis_index("dp")
    m = lax.axis_index("mp")
    return x, s // 4, (s // 2) % 2, s % 2, m


def at(x, y, zl, c, m):
    return (y * 4 + zl * 2 + c, x, m)


def greet(peers):
    barrier = pltpu.get_barrier_semaphore()
    for peer in peers:
        pl.semaphore_signal(barrier, inc=1, device_id=peer, device_id_type=MESH)
    pl.semaphore_wait(barrier, len(peers))


class Copies:
    def __init__(self, send, recv):
        self.send, self.recv, self.all = send, recv, []

    def go(self, src, dst, peer):
        k = len(self.all)
        copy = pltpu.make_async_remote_copy(
            src_ref=src,
            dst_ref=dst,
            send_sem=self.send.at[k],
            recv_sem=self.recv.at[k],
            device_id=peer,
            device_id_type=MESH,
        )
        copy.start()
        self.all.append(copy)
        return copy

    def drain(self):
        for copy in self.all:
            copy.wait_send()


def comm_call(body, ins, outs, copies, cid, limit=40 * 2**20):
    vm = pl.BlockSpec(memory_space=pltpu.VMEM)
    return pl.pallas_call(
        body,
        out_shape=[jax.ShapeDtypeStruct(s, d) for s, d in outs],
        in_specs=[vm] * len(ins),
        out_specs=[vm] * len(outs),
        scratch_shapes=[
            pltpu.SemaphoreType.DMA((copies,)),
            pltpu.SemaphoreType.DMA((copies,)),
        ],
        compiler_params=pltpu.CompilerParams(
            collective_id=cid, has_side_effects=True, vmem_limit_bytes=limit
        ),
    )(*ins)


def heads_kernel(part, fc2, dest, bias, rs, f2p, dall, ball, send, recv):
    x, y, zl, c, m = place()
    s = y * 4 + zl * 2 + c
    across = [(s, x, (m + k) % 4) for k in (2, 1, 3)]
    groups = [
        ((s + i) % 16, (x + j) % 4, m) for i in range(16) for j in range(4) if i or j
    ]
    greet(across + groups)
    cp = Copies(send, recv)
    for peer in across:
        cp.go(part.at[peer[2]], rs.at[m], peer)
    for dy in range(4):
        for dx in range(4):
            if dx or dy:
                px, py = (x + dx) % 4, (y + dy) % 4
                cols = pl.ds(pl.multiple_of((py * 4 + px) * 128, 128), 128)
                cp.go(fc2.at[:, cols], f2p.at[y * 4 + x], at(px, py, zl, c, m))
    for peer in groups:
        cp.go(dest, dall.at[s * 4 + x], peer)
    for dz in range(2):
        for dc in range(2):
            if dz or dc:
                cp.go(bias, ball.at[zl * 2 + c], at(x, y, (zl + dz) % 2, (c + dc) % 2, m))
    rs[m] = part[m]
    mine = y * 4 + x
    f2p[mine] = fc2[:, pl.ds(pl.multiple_of(mine * 128, 128), 128)]
    dall[s * 4 + x] = dest[...]
    ball[zl * 2 + c] = bias[...]
    for copy in cp.all:
        copy.wait_recv()
    cp.drain()


def gather_kernel(cut, blk, col, plane, column, send, recv):
    x, y, zl, c, m = place()
    z = 2 * m + zl
    xs = [(x + k) % 4 for k in range(4)]
    ys = [(y + k) % 4 for k in range(4)]
    zs = [(z + k) % 8 for k in range(8)]

    def zdev(zz, cc):
        return at(x, y, zz % 2, cc, zz // 2)

    right, left = at(xs[1], y, zl, c, m), at(xs[3], y, zl, c, m)
    up, down = at(x, ys[1], zl, c, m), at(x, ys[3], zl, c, m)
    above, below = zdev(zs[1], c), zdev(zs[7], c)
    twin = zdev(z, 1 - c)
    greet([right, left, up, down, above, below, twin])
    cp = Copies(send, recv)

    def block(v, a, b, lo, hi):
        fx, fy = (xs[a], ys[b]) if v == 0 else (xs[b], ys[a])
        return plane.at[2 * v + lo : 2 * v + hi, fy, fx]

    ahead = [[(right, left), (up, down)], [(up, down), (right, left)]]

    def push(v, axis, sgn, a, b, lo=0, hi=2, own=False):
        src = blk.at[2 * v + lo : 2 * v + hi] if own else block(v, a, b, lo, hi)
        return cp.go(src, block(v, a, b, lo, hi), ahead[v][axis][0 if sgn > 0 else 1])

    cpz = {}

    def hop(k):
        if k == 0:
            src = col
            cpz["u", 1] = cp.go(src, column.at[z, c], above)
            cpz["d", 1] = cp.go(src, column.at[z, c], below)
            cpz["t", 0] = cp.go(src, column.at[z, c], twin)
            return
        lo_, hi_ = zs[8 - k], zs[k]
        if k < 4:
            cpz["u", k].wait_recv()
            part = cut(0) if k == 3 else None
            ref = column.at[lo_, c]
            half = ref if part is None else ref.at[part]
            cpz["u", k + 1] = cp.go(half, half, above)
            cpz["t", k] = cp.go(ref, ref, twin)
            cpz["d", k].wait_recv()
            part = cut(1) if k == 3 else None
            ref = column.at[hi_, c]
            half = ref if part is None else ref.at[part]
            cpz["d", k + 1] = cp.go(half, half, below)
            cpz["t", -k] = cp.go(ref, ref, twin)
        else:
            cpz["u", 4].wait_recv()
            cpz["d", 4].wait_recv()
            ref = column.at[zs[4], c]
            cpz["t", 4] = cp.go(ref, ref, twin)

    hop(0)
    one, two, three, four = {}, {}, {}, {}
    for v in range(2):
        for g in (1, -1):
            one[v, g] = push(v, 0, g, 0, 0, own=True)
    for v in range(2):
        for g in (1, -1):
            three[v, 0, g] = push(v, 1, g, 0, 0, own=True)
    column[z, c] = col[...]
    plane[:, y, x] = blk[...]
    for g in (1, -1):
        for v in range(2):
            one[v, g].wait_recv()
            a = -g % 4
            two[v, g] = push(v, 0, g, a, 0, *((0, 1) if g > 0 else (1, 2)))
            for h in (1, -1):
                three[v, a, h] = push(v, 1, h, a, 0)
    hop(1)

    def opposite(a):
        for g in (1, -1):
            for v in range(2):
                three[v, a, g].wait_recv()
                four[v, a, g] = push(v, 1, g, a, -g % 4, *((0, 1) if g > 0 else (1, 2)))

    opposite(0)
    for v in range(2):
        for g in (1, -1):
            two[v, g].wait_recv()
        for h in (1, -1):
            three[v, 2, h] = push(v, 1, h, 2, 0)
    hop(2)
    opposite(3)
    opposite(1)
    hop(3)
    opposite(2)
    hop(4)
    for copy in four.values():
        copy.wait_recv()
    for key, copy in cpz.items():
        if key[0] == "t":
            copy.wait_recv()
    cp.drain()


def owner_kernel(out, emb, send, recv):
    x, y, zl, c, m = place()
    peers = [
        ((x + i) % 4, (y + j) % 4, (m + k) % 4)
        for i in range(4)
        for j in range(4)
        for k in range(4)
        if i or j or k
    ]
    greet([at(px, py, zl, c, pm) for px, py, pm in peers])
    cp = Copies(send, recv)
    mine = (pl.ds(pl.multiple_of(m * 32, 32), 32), pl.ds(pl.multiple_of((y * 4 + x) * 128, 128), 128))

    def rows(px, py):
        return pl.ds(pl.multiple_of((py * 4 + px) * 32, 32), 32)

    for px, py, pm in peers:
        cp.go(out.at[pm, rows(px, py)], emb.at[mine], at(px, py, zl, c, pm))
    emb[mine] = out[m, rows(x, y)]
    for copy in cp.all:
        copy.wait_recv()
    cp.drain()


def rows_kernel(rows, got, send, recv):
    s, d, m = lax.axis_index("section"), lax.axis_index("dp"), lax.axis_index("mp")
    peers = [((s + i) % 16, (d + j) % 4, m) for i in range(16) for j in range(4) if i or j]
    greet(peers)
    cp = Copies(send, recv)
    for peer in peers:
        cp.go(rows.at[peer[0] * 4 + peer[1]], got.at[s * 4 + d], peer)
    got[s * 4 + d] = rows[s * 4 + d]
    for copy in cp.all:
        copy.wait_recv()
    cp.drain()


def squares_kernel(own, every, send, recv):
    s, d, m = lax.axis_index("section"), lax.axis_index("dp"), lax.axis_index("mp")
    peers = [(s, d, (m + k) % 4) for k in (2, 1, 3)]
    greet(peers)
    cp = Copies(send, recv)
    for peer in peers:
        cp.go(own, every.at[m], peer)
    every[m] = own[...]
    for copy in cp.all:
        copy.wait_recv()
    cp.drain()


def layer_norm(values, gain):
    centred = values.astype(F32)
    centred = centred - jnp.mean(centred, axis=-1, keepdims=True)
    variance = jnp.mean(centred * centred, axis=-1, keepdims=True)
    return centred * lax.rsqrt(variance + vit_eps) * gain.astype(F32)


def per_device(
    patches,
    patch_counts,
    dest_rows,
    qkv_weight,
    out_weight,
    attn_gain,
    merge_gain,
    fc1_weight,
    fc1_bias,
    fc2_weight,
    fc2_bias,
    text_embeds,
    section_hidden,
    llm_gain,
):
    width = patches.shape[1]
    tiles, block = 2, 256
    local_cols = qkv_weight.shape[2]
    local_heads = local_cols // HEAD_DIM
    seq_rows = text_embeds.shape[0]
    merged = 128
    section, dp, mp = (lax.axis_index(a) for a in ("section", "dp", "mp"))
    incoming = lax.ppermute(section_hidden, "section", [(k, k + 1) for k in range(15)])

    normed_in = layer_norm(patches, attn_gain).astype(BF)
    projections = jnp.dot(
        normed_in, qkv_weight.reshape(width, 3 * local_cols), preferred_element_type=F32
    ).astype(BF)
    projections = projections.reshape(tiles, block, 3, local_heads, HEAD_DIM)
    query_part, key_part, value_part = (projections[:, :, k] for k in range(3))
    scores = jnp.einsum(
        "tqhd,tkhd->thqk", query_part, key_part, preferred_element_type=F32
    ) * HEAD_DIM ** (-0.5)
    key_live = jnp.arange(block, dtype=jnp.int32)[None, None, None, :] < patch_counts[:, None, None, None]
    scores = jnp.where(key_live, scores, -1e30)
    weights = jax.nn.softmax(scores, axis=-1).astype(BF)
    attended = jnp.einsum(
        "thqk,tkhd->tqhd", weights, value_part, preferred_element_type=F32
    ).astype(BF)
    attended = attended.reshape(patches.shape[0], local_cols)
    partial_proj = jnp.dot(attended, out_weight, preferred_element_type=F32).astype(BF)

    slot_in_tile = jnp.arange(merged, dtype=jnp.int32) % (block // 4)
    tile_counts = jnp.repeat(patch_counts, block // 4, total_repeat_length=merged)
    live = slot_in_tile * 4 < tile_counts
    dest_live = jnp.where(live, dest_rows, 2**30)[None, :]
    rs, f2p, dall, ball = comm_call(
        heads_kernel,
        (
            partial_proj.reshape(4, 128, width),
            fc2_weight,
            dest_live,
            jnp.broadcast_to(fc1_bias[:, None], (80, 128)),
        ),
        [
            ((4, 128, width), BF),
            ((16, 80, 128), BF),
            ((64, 1, 128), jnp.int32),
            ((4, 80, 128), BF),
        ],
        3 + 15 + 63 + 3,
        1,
    )
    own_patches = lax.dynamic_slice_in_dim(patches, mp * 128, 128, 0)
    block_out = (own_patches.astype(F32) + rs.astype(F32).sum(0)).astype(BF)
    merge_part = layer_norm(block_out, merge_gain).astype(BF)
    merge_part = merge_part.reshape(32, 4, width).transpose(1, 0, 2)

    rows_all, fc1_all = comm_call(
        lambda *a: gather_kernel(
            lambda k: (slice(None), slice(640 * k, 640 * (k + 1))), *a
        ),
        (merge_part, fc1_weight.T),
        [((4, 4, 4, 32, width), BF), ((8, 2, 80, width), BF)],
        40 + 16,
        2,
    )
    rows_all = rows_all.reshape(4, 512, width)
    fc1_all = fc1_all.reshape(4, 320, width)
    first = sum(
        lax.dot_general(
            fc1_all[p], rows_all[p], (((1,), (1,)), ((), ())), preferred_element_type=F32
        )
        for p in range(4)
    )
    first = first + ball.reshape(320, 128)[:, :1].astype(F32)
    hidden = jax.nn.gelu(first, approximate=False).astype(BF)

    hidden_all, fc2_all = comm_call(
        lambda *a: gather_kernel(lambda k: (slice(8 * k, 8 * (k + 1)),), *a),
        (hidden.reshape(4, 80, 512), f2p),
        [((4, 4, 4, 80, 512), BF), ((8, 2, 16, 80, 128), BF)],
        40 + 16,
        3,
    )
    hidden_all = hidden_all.reshape(5120, 512)
    fc2_all = fc2_all.reshape(4, 5120, 128)
    second = jnp.stack(
        [
            lax.dot_general(
                hidden_all, fc2_all[k], (((0,), (0,)), ((), ())), preferred_element_type=F32
            ).astype(BF)
            for k in range(4)
        ]
    )
    (embeds,) = comm_call(owner_kernel, (second,), [((128, 2048), BF)], 63, 4)
    embeds = (embeds.astype(F32) + fc2_bias.astype(F32)).astype(BF)

    slot = (dest_rows // seq_rows) * 2 + jnp.arange(merged, dtype=jnp.int32) % 2
    pick = (jnp.arange(merged, dtype=jnp.int32)[:, None] == slot[None, :]).astype(BF)
    send_rows = jnp.dot(pick, embeds, preferred_element_type=F32).astype(BF)
    (got,) = comm_call(
        rows_kernel, (send_rows.reshape(64, 2, 2048),), [((64, 2, 2048), BF)], 63, 5
    )
    own_slice = section * 4 + dp
    dall = dall.reshape(64, 64, 2)
    spots = jnp.where(dall // seq_rows == own_slice, dall % seq_rows, -1).max(axis=1).reshape(128)
    put = jnp.arange(seq_rows, dtype=jnp.int32)[:, None] == spots[None, :]
    hit = jnp.any(put, axis=1, keepdims=True)
    placed = jnp.dot(put.astype(BF), got.reshape(128, 2048), preferred_element_type=F32).astype(BF)
    sequence_embeds = jnp.where(hit, placed, text_embeds)
    entering = jnp.where(section == 0, sequence_embeds, incoming).astype(F32)
    squares = jnp.sum(entering * entering, axis=1)
    (every,) = comm_call(squares_kernel, (squares.reshape(4, 128),), [((4, 4, 128), F32)], 3, 6)
    row_total = every.sum(axis=0).reshape(seq_rows)
    layer_inputs = (
        entering * lax.rsqrt(row_total / HID + llm_eps)[:, None] * llm_gain.astype(F32)
    ).astype(BF)
    return (sequence_embeds, layer_inputs)


def solution(mesh):
    in_specs = (
        P(("section", "dp"), None),
        P(("section", "dp")),
        P(("section", "dp")),
        P(None, None, "mp"),
        P("mp", None),
        P(),
        P(),
        P("mp", ("section", "dp")),
        P(("section", "dp")),
        P(("section", "dp"), "mp"),
        P("mp"),
        P(("section", "dp"), "mp"),
        P(("section", "dp"), "mp"),
        P("mp"),
    )
    out_specs = (P(("section", "dp"), "mp"), P(("section", "dp"), "mp"))
    return jax.shard_map(
        per_device, mesh=mesh, in_specs=in_specs, out_specs=out_specs, check_vma=False
    )
```

time: 326 us -> 217 us (0.67)
  waiting for transfers between devices: 182 us -> 0.01 us
  Pallas kernels: 0 us -> 161 us
  starting transfers between devices: 25.3 us -> 2.18 us
  blocking collectives: 22 us -> 0 us
  local copies, waits for them, and re-layouts: 33.5 us -> 15.3 us
  between operations: 15.8 us -> 1.14 us
  other arithmetic: 16.8 us -> 11.6 us
  matrix products: 29 us -> 25.5 us
    pallas_call x0 -> x6, Pallas kernels: none -> 161 us  [comm_call(): pl.pallas_call(body, out_shape=[jax.ShapeDtypeStruct(s, d) for s, d in ou...]
    psum x1 -> x0, waiting for transfers between devices: 75.5 us -> none  [per_device(): lax.psum(first_partial.astype(jnp.bfloat16), 'mp').astype(jnp.float32)]
    reduce_scatter x1 -> x0, waiting for transfers between devices: 54.7 us -> none  [per_device(): lax.psum_scatter(partial_proj.reshape(merged_rows, 4, width), 'mp', scatt...]
    all_to_all x4 -> x0, waiting for transfers between devices: 38.4 us -> none  [the longest x1 21.2 us: sent_and_summed(): lax.all_to_all(cut_along(value, dim, devices), axis, 0, 0, tiled=True)]
    all_to_all x4 -> x0, starting transfers between devices: 23.3 us -> none  [the longest x1 8.83 us: per_device(): lax.all_to_all(send_rows, ('section', 'dp'), split_axis=0, concat_axis=0,...]
    all_to_all x1 -> x0, blocking collectives: 22 us -> none  [copy_for_each(): return lax.all_to_all(copies, axis, split_axis=0, concat_axis=0, tiled=True)]
    scatter x3 -> x0, local copies, waits for them, and re-layouts: 13.9 us -> none  [the longest x1 7.99 us: per_device(): send_rows = jnp.zeros((group_count, run_cap, feature_cols), jnp.bfloat16)...]
    all_gather x1 -> x0, waiting for transfers between devices: 13.1 us -> none  [gather_turned(): out = lax.all_gather(both, axis, axis=0, tiled=True)]
  transfers between devices with their start and end apart: 8 -> 1, of which waited for: 6 -> 0; matrix products, arithmetic and copies ran while one was open for 10% -> 20% of each run, Pallas kernels for 0% -> 71%
where the time goes in v1:
time: 217 us
  Pallas kernels  161 us (74%)
  matrix products  25.5 us (12%)
  local copies, waits for them, and re-layouts  15.3 us (7%)
  other arithmetic  11.6 us (5%)
  starting transfers between devices  2.18 us (1%)
    pallas_call x6, Pallas kernels, comm_call(): pl.pallas_call(body, out_shape=[jax.ShapeDtypeStruct(s, d) for s, d in ou...  161 us
    dot_general x4, matrix products, per_device(): lax.dot_general(hidden_all, fc2_all[k], (((0,), (0,)), ((), ())), preferr...  6.26 us
    dot_general x4, matrix products, per_device(): lax.dot_general(fc1_all[p], rows_all[p], (((1,), (1,)), ((), ())), prefer...  5.53 us
    dot_general x1, matrix products, per_device(): jnp.dot(put.astype(BF), got.reshape(128, 2048), preferred_element_type=F32)  4.67 us
  transfers between devices with their start and end apart: 1, of which 0 were waited for; matrix products, arithmetic and copies ran while one was open for 20% of the time, Pallas kernels for 71%

profile of v1, /device:TPU:8, one launch (start us, length us, event | category | flops | bytes accessed | tf_op | source)
XLA Modules:
  0.0 216.5 jit_solution(1808806144595250057)
XLA Ops:
  0.7 2.2 %collective-permute-start = (bf16[512,2048]{1,0:T(8,128)(2,1)}, bf16[512,2048]{1,0:T(8,128)(2,1)}, u32[]{:S(2)}, u32[]{:S(2)}) collective-permute-start(bf16[512,2048]{1,0:T(8,128)(2,1)} %param.28), channel_id=1, source_target_pairs={{0,16},{16,32},{32,48},{48,64},{64,80},{80,96},{96,112},{112,128},... | collective-permute-start | bytes 6291464 | tf_op jit(solution)/shard_map/ppermute | solution.py:290
  3.6 1.4 fusion.54
  5.0 1.6 convert_reduce_fusion
  7.1 2.6 %convolution_convert_fusion.3 = bf16[512,960]{0,1:T(8,128)(2,1)} fusion(bf16[1280,960]{0,1:T(8,128)(2,1)S(1)} %bitcast.92, bf16[512,1280]{1,0:T(8,128)(2,1)S(1)} %copy-done.3, f32[1280]{0:T(1024)S(1)} %convert_element_type.85, f32[512]{0:T(512)S(1)} %add_rsqrt_fusion, f32[512]{0:T(512)S(1)} %broadcast_multiply_fusion), kind=kOutput, calls=%fused_computation.23 | convolution fusion | flops 1262059520 | bytes 4760576 | tf_op jit(solution)/shard_map/dot_general | solution.py:293
  9.7 2.7 %reshape.171 = bf16[2,256,3,4,80]{1,0,4,3,2:T(2,128)(2,1)S(1)} reshape(bf16[512,960]{0,1:T(8,128)(2,1)} %convolution_convert_fusion.3) | data formatting | bytes 1966080 | tf_op jit(solution)/shard_map/reshape | solution.py:296
  12.3 1.6 fusion.53
  13.9 3.3 %fusion.55 = (f32[2,4,256]{2,1,0:T(4,128)S(1)}, f32[2,4,256,256]{2,3,1,0:T(8,128)}) fusion(pred[2,256]{1,0:T(4,128)(4,1)S(1)} %iota_compare_fusion.4, bf16[2,256,1,4,80]{1,0,4,3,2:T(2,128)(2,1)} %get-tuple-element.46, bf16[2,256,1,4,80]{1,0,4,3,2:T(2,128)(2,1)} %get-tuple-element.45), kind=kOutput, calls=%fused_computation.115 | convolution fusion | flops 85983488 | bytes 2761216 | tf_op jit(solution)/shard_map/sub | solution.py:303
  17.2 2.0 fusion.16
  21.9 44.2 %shard_map.149 = (bf16[4,128,1280]{2,1,0:T(8,128)(2,1)S(1)}, bf16[16,80,128]{2,1,0:T(8,128)(2,1)S(1)}, s32[64,1,128]{2,1,0:T(1,128)S(1)}, bf16[4,80,128]{2,1,0:T(8,128)(2,1)S(1)}) custom-call(bf16[4,128,1280]{2,1,0:T(8,128)(2,1)S(1)} %bitcast.93, bf16[80,2048]{1,0:T(8,128)(2,1)S(1)} %copy-done.1, s32[1,128]{1,0:T(1,128)S(1)} %get-tuple-element.48.dest, ...), custom_call_target="tpu_custom_call" | custom-call | tf_op jit(solution)/shard_map/pallas_call | solution.py:61
  70.8 33.4 %shard_map.150 = (bf16[4,4,4,32,1280]{4,3,2,1,0:T(8,128)(2,1)S(1)}, bf16[8,2,80,1280]{3,2,1,0:T(8,128)(2,1)S(1)}) custom-call(bf16[4,32,1280]{2,1,0:T(8,128)(2,1)S(1)} %bitcast.94, bf16[80,1280]{1,0:T(8,128)(2,1)S(1)} %bitcast.96), custom_call_target="tpu_custom_call" | custom-call | tf_op jit(solution)/shard_map/pallas_call | solution.py:61
  104.2 2.5 %fusion.51 = (bf16[1,4,4,32,1280]{4,3,2,1,0:T(8,128)(2,1)}, bf16[1,4,4,32,1280]{4,3,2,1,0:T(8,128)(2,1)}, bf16[1,4,4,32,1280]{4,3,2,1,0:T(8,128)(2,1)}, bf16[1,4,4,32,1280]{4,3,2,1,0:T(8,128)(2,1)}) fusion(bf16[4,4,4,32,1280]{4,3,2,1,0:T(8,128)(2,1)S(1)} %get-tuple-element.25), kind=kLoop, calls=%fused_computation.111 | loop fusion | bytes 10485760 | tf_op jit(solution)/shard_map/slice | solution.py:349
  106.7 1.7 fusion.52
  108.5 2.3 %fusion.56 = f32[320,512]{1,0:T(8,128)S(1)} fusion(bf16[320,1280]{1,0:T(8,128)(2,1)} %bitcast.115, bf16[512,1280]{1,0:T(8,128)(2,1)} %bitcast.108), kind=kOutput, calls=%fused_computation.116 | convolution fusion | flops 419430400 | bytes 2785280 | tf_op jit(solution)/shard_map/dot_general | solution.py:348
  113.2 2.0 fusion.31
  115.2 36.0 %shard_map.151 = (bf16[4,4,4,80,512]{4,3,2,1,0:T(8,128)(2,1)S(1)}, bf16[8,2,16,80,128]{4,3,2,1,0:T(8,128)(2,1)S(1)}) custom-call(bf16[4,80,512]{2,1,0:T(8,128)(2,1)S(1)} %bitcast.95, bf16[16,80,128]{2,1,0:T(8,128)(2,1)S(1)} %get-tuple-element.27.a_1_), custom_call_target="tpu_custom_call" | custom-call | tf_op jit(solution)/shard_map/pallas_call | solution.py:61
  152.3 1.6 fusion.17
  153.9 1.6 fusion.18
  155.5 1.6 fusion.19
  157.1 1.6 fusion.20
  158.7 21.6 %shard_map.152 = bf16[128,2048]{1,0:T(8,128)(2,1)S(1)} custom-call(bf16[4,512,128]{2,1,0:T(8,128)(2,1)S(1)} %pad_maximum_fusion.out), custom_call_target="tpu_custom_call" | custom-call | tf_op jit(solution)/shard_map/pallas_call | solution.py:61
  181.0 18.1 %shard_map.153 = bf16[64,2,2048]{2,1,0:T(2,128)(2,1)S(1)} custom-call(bf16[64,2,2048]{2,1,0:T(2,128)(2,1)S(1)} %reshape.179.rows), custom_call_target="tpu_custom_call" | custom-call | tf_op jit(solution)/shard_map/pallas_call | solution.py:61
  200.1 4.7 %fusion.1 = (f32[512]{0:T(512)S(1)}, bf16[512,2048]{1,0:T(8,128)(2,1)}) fusion(bf16[512,2048]{1,0:T(8,128)(2,1)} %collective-permute-done, pred[]{:T(512)S(6)} %eq.55, bf16[512,2048]{1,0:T(8,128)(2,1)} %param.27, bf16[128,2048]{1,0:T(8,128)(2,1)S(1)} %reshape.180, s32[128]{0:T(128)S(1)} %eq.49, pred[512]{0:T(512)(128)(4,1)S(1)} %fusion.41), kind=kOutput, calls=%fused_computation.3 | convolution fusion | flops 274791936 | bytes 6818817 | tf_op jit(solution)/shard_map/dot_general | solution.py:387
  204.8 7.6 %shard_map.154 = f32[4,4,128]{2,1,0:T(4,128)S(1)} custom-call(f32[4,128]{1,0:T(4,128)S(1)} %bitcast.98), custom_call_target="tpu_custom_call" | custom-call | tf_op jit(solution)/shard_map/pallas_call | solution.py:61
  212.4 4.1 %fusion.3 = bf16[512,2048]{1,0:T(8,128)(2,1)} fusion(f32[2048]{0:T(1024)S(1)} %convert_element_type.109, f32[512]{0:T(512)S(1)} %rsqrt_bitcast_fusion, bf16[512,2048]{1,0:T(8,128)(2,1)} %get-tuple-element.54, bf16[512,2048]{1,0:T(8,128)(2,1)} %collective-permute-done, pred[]{:T(512)S(6)} %eq.55), kind=kLoop, calls=%fused_computation.5 | loop fusion | flops 5242880 | bytes 6301697 | tf_op jit(solution)/shard_map/convert_element_type | solution.py:395
  (76 shorter events, 13.8 us)
Async XLA Ops:
  0.6 6.4 %copy-start = (bf16[1280,3,320]{0,2,1:T(8,128)(2,1)S(1)}, bf16[1280,3,320]{0,2,1:T(8,128)(2,1)}, u32[]{:S(2)}) copy-start(bf16[1280,3,320]{0,2,1:T(8,128)(2,1)} %param.19) | copy-start | bytes 7372804
  0.6 5.9 %copy-start.3 = (bf16[512,1280]{1,0:T(8,128)(2,1)S(1)}, bf16[512,1280]{1,0:T(8,128)(2,1)}, u32[]{:S(2)}) copy-start(bf16[512,1280]{1,0:T(8,128)(2,1)} %param.16) | copy-start | bytes 3932164
  0.7 6.4 %copy-start.11 = (bf16[1280]{0:T(1024)(128)(2,1)S(1)}, bf16[1280]{0:T(1024)(128)(2,1)}, u32[]{:S(2)}) copy-start(bf16[1280]{0:T(1024)(128)(2,1)} %param.21) | copy-start | bytes 7684
  0.7 199.5 %collective-permute-start = (bf16[512,2048]{1,0:T(8,128)(2,1)}, bf16[512,2048]{1,0:T(8,128)(2,1)}, u32[]{:S(2)}, u32[]{:S(2)}) collective-permute-start(bf16[512,2048]{1,0:T(8,128)(2,1)} %param.28), channel_id=1, source_target_pairs={{0,16},{16,32},{32,48},{48,64},{64,80},{80,96},{96,112},{112,128},... | collective-permute-start | bytes 6291464 | tf_op jit(solution)/shard_map/ppermute | solution.py:290
  13.9 3.3 %copy-start.10 = (bf16[2,256,1,4,80]{1,0,4,3,2:T(2,128)(2,1)S(1)}, bf16[2,256,1,4,80]{1,0,4,3,2:T(2,128)(2,1)}, u32[]{:S(2)}) copy-start(bf16[2,256,1,4,80]{1,0,4,3,2:T(2,128)(2,1)} %get-tuple-element.44) | copy-start | bytes 983044
  17.2 2.4 %copy-start.18 = (bf16[320,1280]{1,0:T(8,128)(2,1)S(1)}, bf16[320,1280]{1,0:T(8,128)(2,1)}, u32[]{:S(2)}) copy-start(bf16[320,1280]{1,0:T(8,128)(2,1)} %param.20) | copy-start | bytes 2457604
  19.2 1.3 copy-start.15
  19.2 1.3 copy-start.16
  19.2 2.6 %copy-start.17 = (bf16[80]{0:T(256)(128)(2,1)S(1)}, bf16[80]{0:T(256)(128)(2,1)}, u32[]{:S(2)}) copy-start(bf16[80]{0:T(256)(128)(2,1)} %param.24) | copy-start | bytes 484
  19.2 2.7 %copy-start.1 = (bf16[80,2048]{1,0:T(8,128)(2,1)S(1)}, bf16[80,2048]{1,0:T(8,128)(2,1)}, u32[]{:S(2)}) copy-start(bf16[80,2048]{1,0:T(8,128)(2,1)} %fc2.1) | copy-start | bytes 983044
  66.1 2.7 %copy-start.12 = (bf16[1280]{0:T(1024)(128)(2,1)S(1)}, bf16[1280]{0:T(1024)(128)(2,1)}, u32[]{:S(2)}) copy-start(bf16[1280]{0:T(1024)(128)(2,1)} %param.22) | copy-start | bytes 7684
  67.1 3.7 %copy-start.2 = (bf16[1280,80]{0,1:T(8,128)(2,1)S(1)}, bf16[1280,80]{0,1:T(8,128)(2,1)}, u32[]{:S(2)}) copy-start(bf16[1280,80]{0,1:T(8,128)(2,1)} %param.23) | copy-start | bytes 614404
  108.5 2.4 %copy-start.5 = (bf16[1,4,4,32,1280]{4,3,2,1,0:T(8,128)(2,1)S(1)}, bf16[1,4,4,32,1280]{4,3,2,1,0:T(8,128)(2,1)}, u32[]{:S(2)}) copy-start(bf16[1,4,4,32,1280]{4,3,2,1,0:T(8,128)(2,1)} %get-tuple-element.38) | copy-start | bytes 3932164
  108.5 2.4 %copy-start.7 = (bf16[2,2,80,1280]{3,2,1,0:T(8,128)(2,1)S(1)}, bf16[2,2,80,1280]{3,2,1,0:T(8,128)(2,1)}, u32[]{:S(2)}) copy-start(bf16[2,2,80,1280]{3,2,1,0:T(8,128)(2,1)} %get-tuple-element.42) | copy-start | bytes 2457604
  110.9 1.3 copy-start.4
  110.9 1.5 copy-start.6
  111.5 1.5 copy-start.8
  111.5 1.7 copy-start.9
  158.6 21.7 %copy-start.13 = (bf16[2048]{0:T(1024)(128)(2,1)S(1)}, bf16[2048]{0:T(1024)(128)(2,1)}, u32[]{:S(2)}) copy-start(bf16[2048]{0:T(1024)(128)(2,1)} %param.26) | copy-start | bytes 12292
  180.3 19.6 %copy-start.14 = (bf16[2048]{0:T(1024)(128)(2,1)S(1)}, bf16[2048]{0:T(1024)(128)(2,1)}, u32[]{:S(2)}) copy-start(bf16[2048]{0:T(1024)(128)(2,1)} %param.29) | copy-start | bytes 12292

commit v2 on v0

v2 whole, which is shorter than its diff:
```python
import jax
import jax.numpy as jnp
from jax import lax
from jax.experimental import pallas as pl
from jax.experimental.pallas import tpu as pltpu
from jax.sharding import PartitionSpec as P

HEAD_DIM = 80
HID = 8192
MESH = pl.DeviceIdType.MESH
BF = jnp.bfloat16
F32 = jnp.float32

vit_eps = 1e-06
llm_eps = 1e-06


def place():
    s = lax.axis_index("section")
    x = lax.axis_index("dp")
    m = lax.axis_index("mp")
    return x, s // 4, (s // 2) % 2, s % 2, m


def at(x, y, zl, c, m):
    return (y * 4 + zl * 2 + c, x, m)


def greet(peers):
    barrier = pltpu.get_barrier_semaphore()
    for peer in peers:
        pl.semaphore_signal(barrier, inc=1, device_id=peer, device_id_type=MESH)
    pl.semaphore_wait(barrier, len(peers))


class Copies:
    def __init__(self, send, recv):
        self.send, self.recv, self.all = send, recv, []

    def go(self, src, dst, peer):
        k = len(self.all)
        copy = pltpu.make_async_remote_copy(
            src_ref=src,
            dst_ref=dst,
            send_sem=self.send.at[k],
            recv_sem=self.recv.at[k],
            device_id=peer,
            device_id_type=MESH,
        )
        copy.start()
        self.all.append(copy)
        return copy

    def drain(self):
        for copy in self.all:
            copy.wait_send()


def column_gather(cp, cut, col, column, pos):
    x, y, zl, c, m = pos
    z = 2 * m + zl
    zs = [(z + k) % 8 for k in range(8)]

    def zdev(zz, cc):
        return at(x, y, zz % 2, cc, zz // 2)

    above, below, twin = zdev(zs[1], c), zdev(zs[7], c), zdev(z, 1 - c)
    up, down, side = {}, {}, []

    def hop(k):
        if k == 0:
            up[1] = cp.go(col, column.at[z, c], above)
            down[1] = cp.go(col, column.at[z, c], below)
            side.append(cp.go(col, column.at[z, c], twin))
        elif k < 4:
            for ways, z_from, peer, part in ((up, zs[8 - k], above, 0), (down, zs[k], below, 1)):
                ways[k].wait_recv()
                ref = column.at[z_from, c]
                half = ref.at[cut(part)] if k == 3 else ref
                ways[k + 1] = cp.go(half, half, peer)
                side.append(cp.go(ref, ref, twin))
        else:
            up[4].wait_recv()
            down[4].wait_recv()
            ref = column.at[zs[4], c]
            side.append(cp.go(ref, ref, twin))

    def finish():
        for copy in side:
            copy.wait_recv()

    return hop, finish


def plane_gather(cp, blk, plane, hop, pos):
    x, y, zl, c, m = pos
    xs = [(x + k) % 4 for k in range(4)]
    ys = [(y + k) % 4 for k in range(4)]
    right, left = at(xs[1], y, zl, c, m), at(xs[3], y, zl, c, m)
    up, down = at(x, ys[1], zl, c, m), at(x, ys[3], zl, c, m)
    ahead = [[(right, left), (up, down)], [(up, down), (right, left)]]

    def block(v, a, b, lo, hi):
        fx, fy = (xs[a], ys[b]) if v == 0 else (xs[b], ys[a])
        return plane.at[2 * v + lo : 2 * v + hi, fy, fx]

    def push(v, axis, sgn, a, b, lo=0, hi=2, own=False):
        src = blk.at[2 * v + lo : 2 * v + hi] if own else block(v, a, b, lo, hi)
        return cp.go(src, block(v, a, b, lo, hi), ahead[v][axis][0 if sgn > 0 else 1])

    one, two, three, four = {}, {}, {}, {}
    for v in range(2):
        for g in (1, -1):
            one[v, g] = push(v, 0, g, 0, 0, own=True)
    for v in range(2):
        for g in (1, -1):
            three[v, 0, g] = push(v, 1, g, 0, 0, own=True)
    hop(0)
    plane[:, y, x] = blk[...]
    for g in (1, -1):
        for v in range(2):
            one[v, g].wait_recv()
            a = -g % 4
            two[v, g] = push(v, 0, g, a, 0, *((0, 1) if g > 0 else (1, 2)))
            for h in (1, -1):
                three[v, a, h] = push(v, 1, h, a, 0)
    hop(1)

    def opposite(a):
        for g in (1, -1):
            for v in range(2):
                three[v, a, g].wait_recv()
                four[v, a, g] = push(v, 1, g, a, -g % 4, *((0, 1) if g > 0 else (1, 2)))

    opposite(0)
    for v in range(2):
        for g in (1, -1):
            two[v, g].wait_recv()
        for h in (1, -1):
            three[v, 2, h] = push(v, 1, h, 2, 0)
    hop(2)
    opposite(3)
    opposite(1)
    hop(3)
    opposite(2)
    hop(4)
    for copy in four.values():
        copy.wait_recv()


NT = (((1,), (1,)), ((), ()))
TN = (((0,), (0,)), ((), ()))


def dot(a, b, dims=(((1,), (0,)), ((), ()))):
    return lax.dot_general(a, b, dims, preferred_element_type=F32)


def normed(v, gain):
    v = v - jnp.mean(v, axis=-1, keepdims=True)
    return v * lax.rsqrt(jnp.mean(v * v, axis=-1, keepdims=True) + vit_eps) * gain


def step_kernel(
    patches, key_bias, wqkv, wout, attn_gain, merge_gain, fc1, fc1_bias, fc2, fc2_bias,
    dest, pick, llm_gain, text_hbm, hidden_hbm,
    seq_out, layer_out,
    text, incoming, xn, att, attr, wout_all, f2p, dall, ball, nrm, turn, blk1, rows_all, fc1_all,
    blk2, hid_all, fc2_all, acc, second, emb, flat, send_rows, got, sq_own, sq_all,
    send, recv, send3, recv3, local, relay_send, relay_recv,
):
    pos = place()
    x, y, zl, c, m = pos
    s = y * 4 + zl * 2 + c
    z = 2 * m + zl
    mine = y * 4 + x
    across = [(s, x, (m + k) % 4) for k in (2, 1, 3)]
    groups = [((s + i) % 16, (x + j) % 4, m) for i in range(16) for j in range(4) if i or j]
    owners = [
        ((x + i) % 4, (y + j) % 4, (m + k) % 4)
        for i in range(4) for j in range(4) for k in range(4) if i or j or k
    ]
    barrier = pltpu.get_barrier_semaphore()
    cross = [
        at((x + i) % 4, (y + j) % 4, zl, c, (m + k) % 4)
        for i in range(4) for j in range(4) for k in range(1, 4) if i or j
    ]
    column = [at(x, y, 1 - zl, c, (m + 1) % 4), at(x, y, 1 - zl, c, (m + 3) % 4)]
    peers = across + groups + cross + column
    for peer in peers:
        pl.semaphore_signal(barrier, inc=1, device_id=peer, device_id_type=MESH)

    own_text = pltpu.make_async_copy(text_hbm, text, local.at[0])
    own_text.start()

    gain1 = attn_gain[...].astype(F32)

    def norm_rows(i, carry):
        r = pl.ds(pl.multiple_of(i * 32, 32), 32)
        xn[r, :] = normed(patches[r, :].astype(F32), gain1).astype(BF)
        return carry

    lax.fori_loop(0, 16, norm_rows, 0)
    pl.semaphore_wait(barrier, len(peers))

    cp = Copies(send, recv)
    half_rows = pl.ds(pl.multiple_of((zl * 2 + c) * 80, 16), 80)
    hop0, finish0 = column_gather(
        cp, lambda k: (slice(None), slice(640 * k, 640 * (k + 1))), wout.at[half_rows], wout_all, pos
    )
    hop0(0)
    wout_all[z, c] = wout[half_rows, :]
    pieces, notes, biases = [], [], []
    for dy in range(4):
        for dx in range(4):
            if dx or dy:
                px, py = (x + dx) % 4, (y + dy) % 4
                cols = pl.ds(pl.multiple_of((py * 4 + px) * 128, 128), 128)
                pieces.append(cp.go(fc2.at[:, cols], f2p.at[mine], at(px, py, zl, c, m)))
    for peer in groups:
        spot = dall.at[pl.ds(pl.multiple_of((s * 4 + x) * 8, 8), 8)]
        notes.append(cp.go(dest, spot, peer))
    for dz in range(2):
        for dc in range(2):
            if dz or dc:
                biases.append(
                    cp.go(fc1_bias, ball.at[zl * 2 + c], at(x, y, (zl + dz) % 2, (c + dc) % 2, m))
                )
    f2p[mine] = fc2[:, pl.ds(pl.multiple_of(mine * 128, 128), 128)]
    dall[pl.ds(pl.multiple_of((s * 4 + x) * 8, 8), 8), :] = dest[...]
    ball[zl * 2 + c] = fc1_bias[...]

    lane = lax.broadcasted_iota(jnp.int32, (256, 320), 1)
    for t in range(2):
        xt = xn[256 * t : 256 * (t + 1), :]
        q, k, v = (dot(xt, wqkv[j], NT).astype(BF) for j in range(3))
        hop0(2 * t + 1)
        out = jnp.zeros((256, 320), F32)
        for h in range(4):
            inside = (lane >= 80 * h) & (lane < 80 * (h + 1))
            sc = dot(jnp.where(inside, q, jnp.zeros_like(q)), k, NT) * HEAD_DIM ** (-0.5)
            sc = sc + key_bias[t]
            sc = jnp.exp(sc - jnp.max(sc, axis=1, keepdims=True))
            w = (sc / jnp.sum(sc, axis=1, keepdims=True)).astype(BF)
            out = jnp.where(inside, dot(w, v), out)
            if h == 1:
                hop0(2 * t + 2)
        att[2 * t : 2 * t + 2] = out.astype(BF).reshape(2, 128, 320)
    parts = [cp.go(att.at[peer[2]], attr.at[m], peer) for peer in across]
    attr[m] = att[m]
    finish0()
    for copy in parts:
        copy.wait_recv()
    for k in range(4):
        w = wout_all[2 * k : 2 * k + 2].reshape(320, 1280)
        part = dot(attr[k], w)
        nrm[...] = part if k == 0 else nrm[...] + part
    gain2 = merge_gain[...].astype(F32)
    for i in range(4):
        r = pl.ds(pl.multiple_of(m * 128 + 32 * i, 32), 32)
        o = (patches[r, :].astype(F32) + nrm[32 * i : 32 * (i + 1), :]).astype(BF)
        o = normed(o.astype(F32), gain2)
        for b in range(10):
            turn[b, 32 * i : 32 * (i + 1), :] = o[:, 128 * b : 128 * (b + 1)]
    for p in range(4):
        for b in range(10):
            cols = slice(128 * b, 128 * (b + 1))
            blk1[p, :, cols] = turn[b, pl.ds(p, 32, stride=4), :].astype(BF)

    hop1, finish1 = column_gather(
        cp, lambda k: (slice(None), slice(640 * k, 640 * (k + 1))), fc1, fc1_all, pos
    )
    fc1_all[z, c] = fc1[...]
    plane_gather(cp, blk1, rows_all, hop1, pos)
    finish1()
    for copy in biases:
        copy.wait_recv()
    for p in range(4):
        part = dot(
            fc1_all[2 * p : 2 * p + 2].reshape(320, 1280), rows_all[p].reshape(512, 1280), NT
        )
        acc[0:320, :] = part if p == 0 else acc[0:320, :] + part
    for b in range(4):
        h = acc[80 * b : 80 * (b + 1), :] + ball[b][:, :1].astype(F32)
        blk2[b] = (0.5 * h * (1.0 + lax.erf(h * 0.5**0.5))).astype(BF)

    for copy in pieces:
        copy.wait_recv()
    hop2, finish2 = column_gather(
        cp, lambda k: (slice(8 * k, 8 * (k + 1)),), f2p, fc2_all, pos
    )
    fc2_all[z, c] = f2p[...]
    plane_gather(cp, blk2, hid_all, hop2, pos)
    finish2()

    onward = pltpu.make_async_remote_copy(
        src_ref=hidden_hbm, dst_ref=incoming, send_sem=relay_send, recv_sem=relay_recv,
        device_id=((s + 1) % 16, x, m), device_id_type=MESH,
    )

    @pl.when(s < 15)
    def _():
        onward.start()

    for b in range(4):
        zl_, c_ = b // 2, b % 2
        w = jnp.concatenate(
            [fc2_all[2 * k + zl_, c_].reshape(1280, 128) for k in range(4)], axis=1
        )
        part = dot(hid_all[b].reshape(1280, 512), w, TN)
        acc[...] = part if b == 0 else acc[...] + part
    for k in range(4):
        second[k] = acc[:, 128 * k : 128 * (k + 1)].astype(BF)

    cp3 = Copies(send3, recv3)

    def rows(px, py):
        return pl.ds(pl.multiple_of((py * 4 + px) * 32, 32), 32)

    home = (pl.ds(pl.multiple_of(m * 32, 32), 32), pl.ds(pl.multiple_of(mine * 128, 128), 128))
    moved = [
        cp3.go(second.at[pm, rows(px, py)], emb.at[home], at(px, py, zl, c, pm))
        for px, py, pm in owners
    ]
    emb[home] = second[m, rows(x, y)]
    for copy in moved:
        copy.wait_recv()
    bias2 = fc2_bias[...].astype(F32)
    for b in range(16):
        e = (emb[:, 128 * b : 128 * (b + 1)].astype(F32) + bias2[:, 128 * b : 128 * (b + 1)]).astype(BF)
        flat[pl.ds(b, 128, stride=16), :] = dot(pick[...], e)
    send_rows[...] = flat[...].astype(BF).reshape(64, 32, 128)
    moved = [
        cp3.go(send_rows.at[peer[0] * 4 + peer[1]], got.at[s * 4 + x], peer) for peer in groups
    ]
    got[s * 4 + x] = send_rows[s * 4 + x]
    for copy in notes:
        copy.wait_recv()
    d = dall[pl.ds(0, 64, stride=8), :]
    low = (s * 4 + x) * 512
    row = lax.broadcasted_iota(jnp.int32, (64, 512), 1)
    odd = lax.broadcasted_iota(jnp.int32, (64, 128), 1) % 2
    here = (d >= low) & (d < low + 512)
    puts = []
    for i in range(2):
        spot = jnp.max(jnp.where(here & (odd == i), (d - low).astype(F32), -1.0), axis=1, keepdims=True)
        puts.append((row == spot.astype(jnp.int32)).astype(F32).astype(BF))
    own_text.wait()

    @pl.when(s < 15)
    def _():
        onward.wait_send()

    @pl.when(s > 0)
    def _():
        onward.wait_recv()

    for copy in moved:
        copy.wait_recv()
    flat[...] = got[...].reshape(2048, 128).astype(F32)
    ones = jnp.ones((64, 128), BF)
    first = s == 0
    squares = [jnp.zeros((128, 128), F32) for _ in range(4)]
    hits = [
        dot(puts[0][:, 128 * r : 128 * (r + 1)], ones, TN)
        + dot(puts[1][:, 128 * r : 128 * (r + 1)], ones, TN)
        for r in range(4)
    ]
    for b in range(16):
        new = [flat[pl.ds(16 * i + b, 64, stride=32), :].astype(BF) for i in range(2)]
        cols = slice(128 * b, 128 * (b + 1))
        for r in range(4):
            rr = slice(128 * r, 128 * (r + 1))
            placed = dot(puts[0][:, rr], new[0], TN) + dot(puts[1][:, rr], new[1], TN)
            seq = jnp.where(hits[r] > 0.5, placed, text[rr, cols].astype(F32))
            seq_out[rr, cols] = seq.astype(BF)
            enter = jnp.where(first, seq, incoming[rr, cols].astype(F32))
            squares[r] = squares[r] + enter * enter
    sub = lax.broadcasted_iota(jnp.int32, (8, 128), 0)
    total = jnp.zeros((8, 128), F32)
    for r in range(4):
        line = jnp.broadcast_to(jnp.sum(squares[r], axis=1, keepdims=True), (128, 128)).T
        total = jnp.where(sub == r, line[0:8], total)
    sq_own[...] = total
    moved = [cp3.go(sq_own, sq_all.at[m], peer) for peer in across]
    sq_all[m] = total
    for copy in moved:
        copy.wait_recv()
    total = (sq_all[0] + sq_all[1]) + (sq_all[2] + sq_all[3])
    scale = lax.rsqrt(total / HID + llm_eps)
    gain3 = llm_gain[...].astype(F32)
    for r in range(4):
        by = jnp.broadcast_to(scale[r : r + 1, :], (128, 128)).T
        rr = slice(128 * r, 128 * (r + 1))
        for b in range(16):
            cols = slice(128 * b, 128 * (b + 1))
            enter = jnp.where(first, seq_out[rr, cols].astype(F32), incoming[rr, cols].astype(F32))
            layer_out[rr, cols] = (enter * by * gain3[:, cols]).astype(BF)
    cp.drain()
    cp3.drain()


def per_device(
    patches, patch_counts, dest_rows, qkv_weight, out_weight, attn_gain, merge_gain,
    fc1_weight, fc1_bias, fc2_weight, fc2_bias, text_embeds, section_hidden, llm_gain,
):
    merged, seq_rows = 128, text_embeds.shape[0]
    slot_in_tile = jnp.arange(merged, dtype=jnp.int32) % 64
    live = slot_in_tile * 4 < jnp.repeat(patch_counts, 64, total_repeat_length=merged)
    dest_live = jnp.broadcast_to(jnp.where(live, dest_rows, 2**30)[None, :], (8, merged))
    key_live = jnp.arange(256, dtype=jnp.int32)[None, None, :] < patch_counts[:, None, None]
    key_bias = jnp.where(key_live, 0.0, -1e30).astype(F32)
    slot = (dest_rows // seq_rows) * 2 + jnp.arange(merged, dtype=jnp.int32) % 2
    pick = (jnp.arange(merged, dtype=jnp.int32)[:, None] == slot[None, :]).astype(BF)
    vm = pl.BlockSpec(memory_space=pltpu.VMEM)
    hbm = pl.BlockSpec(memory_space=pl.ANY)
    dma = pltpu.SemaphoreType.DMA
    first_copies = 16 + 15 + 63 + 3 + 3 + 56 + 56
    return pl.pallas_call(
        step_kernel,
        out_shape=[jax.ShapeDtypeStruct((512, 2048), BF)] * 2,
        in_specs=[vm] * 13 + [hbm] * 2,
        out_specs=[vm] * 2,
        scratch_shapes=[
            pltpu.VMEM((512, 2048), BF),
            pltpu.VMEM((512, 2048), BF),
            pltpu.VMEM((512, 1280), BF),
            pltpu.VMEM((4, 128, 320), BF),
            pltpu.VMEM((4, 128, 320), BF),
            pltpu.VMEM((8, 2, 80, 1280), BF),
            pltpu.VMEM((16, 80, 128), BF),
            pltpu.VMEM((512, 128), jnp.int32),
            pltpu.VMEM((4, 80, 128), BF),
            pltpu.VMEM((128, 1280), F32),
            pltpu.VMEM((10, 128, 128), F32),
            pltpu.VMEM((4, 32, 1280), BF),
            pltpu.VMEM((4, 4, 4, 32, 1280), BF),
            pltpu.VMEM((8, 2, 80, 1280), BF),
            pltpu.VMEM((4, 80, 512), BF),
            pltpu.VMEM((4, 4, 4, 80, 512), BF),
            pltpu.VMEM((8, 2, 16, 80, 128), BF),
            pltpu.VMEM((512, 512), F32),
            pltpu.VMEM((4, 512, 128), BF),
            pltpu.VMEM((128, 2048), BF),
            pltpu.VMEM((2048, 128), F32),
            pltpu.VMEM((64, 32, 128), BF),
            pltpu.VMEM((64, 32, 128), BF),
            pltpu.VMEM((8, 128), F32),
            pltpu.VMEM((4, 8, 128), F32),
            dma((first_copies,)),
            dma((first_copies,)),
            dma((63 + 63 + 3,)),
            dma((63 + 63 + 3,)),
            dma((1,)),
            dma,
            dma,
        ],
        compiler_params=pltpu.CompilerParams(
            collective_id=1, has_side_effects=True, vmem_limit_bytes=60 * 2**20
        ),
    )(
        patches,
        key_bias,
        qkv_weight.transpose(1, 2, 0),
        out_weight,
        attn_gain[None, :],
        merge_gain[None, :],
        fc1_weight.T,
        jnp.broadcast_to(fc1_bias[:, None], (80, 128)),
        fc2_weight,
        fc2_bias[None, :],
        dest_live,
        pick,
        llm_gain[None, :],
        text_embeds,
        section_hidden,
    )


def solution(mesh):
    in_specs = (
        P(("section", "dp"), None),
        P(("section", "dp")),
        P(("section", "dp")),
        P(None, None, "mp"),
        P("mp", None),
        P(),
        P(),
        P("mp", ("section", "dp")),
        P(("section", "dp")),
        P(("section", "dp"), "mp"),
        P("mp"),
        P(("section", "dp"), "mp"),
        P(("section", "dp"), "mp"),
        P("mp"),
    )
    out_specs = (P(("section", "dp"), "mp"), P(("section", "dp"), "mp"))
    return jax.shard_map(
        per_device, mesh=mesh, in_specs=in_specs, out_specs=out_specs, check_vma=False
    )
```

time: 326 us -> 201 us (0.62)
  Pallas kernels: 0 us -> 182 us
  waiting for transfers between devices: 182 us -> 0 us
  matrix products: 29 us -> 0 us
  starting transfers between devices: 25.3 us -> 0 us
  blocking collectives: 22 us -> 0 us
  local copies, waits for them, and re-layouts: 33.5 us -> 13 us
  between operations: 15.8 us -> 0.65 us
  other arithmetic: 16.8 us -> 3.89 us
    pallas_call x0 -> x1, Pallas kernels: none -> 182 us  [per_device(): pl.pallas_call(step_kernel, out_shape=[jax.ShapeDtypeStruct((512, 2048),...]
    psum x1 -> x0, waiting for transfers between devices: 75.5 us -> none  [per_device(): lax.psum(first_partial.astype(jnp.bfloat16), 'mp').astype(jnp.float32)]
    reduce_scatter x1 -> x0, waiting for transfers between devices: 54.7 us -> none  [per_device(): lax.psum_scatter(partial_proj.reshape(merged_rows, 4, width), 'mp', scatt...]
    all_to_all x4 -> x0, waiting for transfers between devices: 38.4 us -> none  [the longest x1 21.2 us: sent_and_summed(): lax.all_to_all(cut_along(value, dim, devices), axis, 0, 0, tiled=True)]
    dot_general x5 -> x0, matrix products: 25.7 us -> none  [the longest x1 12.3 us: per_device(): jnp.dot(hidden, second_full, preferred_element_type=jnp.float32)]
    all_to_all x4 -> x0, starting transfers between devices: 23.3 us -> none  [the longest x1 8.83 us: per_device(): lax.all_to_all(send_rows, ('section', 'dp'), split_axis=0, concat_axis=0,...]
    all_to_all x1 -> x0, blocking collectives: 22 us -> none  [copy_for_each(): return lax.all_to_all(copies, axis, split_axis=0, concat_axis=0, tiled=True)]
    scatter x3 -> x0, local copies, waits for them, and re-layouts: 13.9 us -> none  [the longest x1 7.99 us: per_device(): send_rows = jnp.zeros((group_count, run_cap, feature_cols), jnp.bfloat16)...]
  transfers between devices with their start and end apart: 8 -> 0, of which waited for: 6 -> 0; matrix products, arithmetic and copies ran while one was open for 10% -> 0% of each run, Pallas kernels for 0% -> 0%
where the time goes in v2:
time: 201 us; the launch traced here: 199 us
  Pallas kernels  182 us (91%)
  local copies, waits for them, and re-layouts  13 us (6%)
  other arithmetic  3.89 us (2%)
    pallas_call x1, Pallas kernels, per_device(): pl.pallas_call(step_kernel, out_shape=[jax.ShapeDtypeStruct((512, 2048),...  182 us
    unnamed x4, local copies, waits for them, and re-layouts  4.63 us

profile of v2, /device:TPU:8, one launch (start us, length us, event | category | flops | bytes accessed | tf_op | source)
XLA Modules:
  0.0 199.3 jit_solution(2655058570913180727)
XLA Ops:
  0.6 1.3 fusion.3
  1.9 2.0 fusion.1
  3.9 1.3 compare_select_fusion.key_bias
  5.2 0.6 broadcast_in_dim.53.dest
  5.8 1.3 broadcast_in_dim.48.attn_gain
  7.1 1.3 broadcast_in_dim.49.merge_gain
  8.4 1.3 broadcast_in_dim.51.fc2_bias
  9.6 1.3 broadcast_in_dim.54.llm_gain
  10.9 1.3 broadcast_in_dim.50.fc1_bias
  12.3 0.6 fusion.pick
  12.9 181.8 %shard_map.149 = (bf16[512,2048]{1,0:T(8,128)(2,1)}, bf16[512,2048]{1,0:T(8,128)(2,1)}) custom-call(bf16[512,1280]{1,0:T(8,128)(2,1)} %patches.1, f32[2,1,256]{2,1,0:T(1,128)} %compare_select_fusion.key_bias, bf16[3,320,1280]{2,1,0:T(8,128)(2,1)} %bitcast.4, bf16[320,1280]{1,0:T(8,128)(2,1)} %wout.1, bf16[1,1280]{1,0:T(2,128)(2,1)} %broadcast_in_dim.48.attn_gain, ...), custom_call_target="tpu_custom_call" | custom-call | tf_op jit(solution)/shard_map/pallas_call | solution.py:419
  194.7 0.0 copy-start
  194.7 3.3 %copy.18 = bf16[512,2048]{1,0:T(8,128)(2,1)} copy(bf16[512,2048]{1,0:T(8,128)(2,1)} %get-tuple-element.20) | data formatting | bytes 4194304
  198.0 0.0 copy-done
  198.0 1.3 copy.19
Async XLA Ops:
  194.7 3.3 %copy-start = (bf16[512,2048]{1,0:T(8,128)(2,1)S(1)}, bf16[512,2048]{1,0:T(8,128)(2,1)}, u32[]{:S(2)}) copy-start(bf16[512,2048]{1,0:T(8,128)(2,1)} %get-tuple-element.21) | copy-start | bytes 6291460

commit v3 on v2

--- a/solution.py
+++ b/solution.py
@@ -56,7 +56,7 @@
             copy.wait_send()
 
 
-def column_gather(cp, cut, col, column, pos):
+def column_gather(cp, halves, col, column, pos):
     x, y, zl, c, m = pos
     z = 2 * m + zl
     zs = [(z + k) % 8 for k in range(8)]
@@ -69,20 +69,21 @@
 
     def hop(k):
         if k == 0:
-            up[1] = cp.go(col, column.at[z, c], above)
-            down[1] = cp.go(col, column.at[z, c], below)
+            for j in range(2):
+                src, dst = col.at[halves[j]], column.at[z, c].at[halves[j]]
+                up[1, j] = cp.go(src, dst, above)
+                down[1, j] = cp.go(src, dst, below)
             side.append(cp.go(col, column.at[z, c], twin))
-        elif k < 4:
-            for ways, z_from, peer, part in ((up, zs[8 - k], above, 0), (down, zs[k], below, 1)):
-                ways[k].wait_recv()
-                ref = column.at[z_from, c]
-                half = ref.at[cut(part)] if k == 3 else ref
-                ways[k + 1] = cp.go(half, half, peer)
-                side.append(cp.go(ref, ref, twin))
-        else:
-            up[4].wait_recv()
-            down[4].wait_recv()
-            ref = column.at[zs[4], c]
+            return
+        for j in range(2):
+            for ways, z_from, peer, last in ((up, zs[8 - k], above, 0), (down, zs[k % 8], below, 1)):
+                if k < 4 or j == last:
+                    ways[k, j].wait_recv()
+                if k < 3 or (k == 3 and j == last):
+                    ref = column.at[z_from, c].at[halves[j]]
+                    ways[k + 1, j] = cp.go(ref, ref, peer)
+        for z_from in [zs[8 - k], zs[k]][: 2 if k < 4 else 1]:
+            ref = column.at[z_from, c]
             side.append(cp.go(ref, ref, twin))
 
     def finish():
@@ -92,7 +93,7 @@
     return hop, finish
 
 
-def plane_gather(cp, blk, plane, hop, pos):
+def plane_gather(cp, blk, plane, hop, drip, first, pos):
     x, y, zl, c, m = pos
     xs = [(x + k) % 4 for k in range(4)]
     ys = [(y + k) % 4 for k in range(4)]
@@ -125,6 +126,7 @@
             for h in (1, -1):
                 three[v, a, h] = push(v, 1, h, a, 0)
     hop(1)
+    drip(first + 0)
 
     def opposite(a):
         for g in (1, -1):
@@ -139,15 +141,19 @@
         for h in (1, -1):
             three[v, 2, h] = push(v, 1, h, 2, 0)
     hop(2)
+    drip(first + 1)
     opposite(3)
     opposite(1)
     hop(3)
+    drip(first + 2)
     opposite(2)
     hop(4)
+    drip(first + 3)
     for copy in four.values():
         copy.wait_recv()
 
 
+BY_ROWS = (slice(0, 48), slice(48, 80))
 NT = (((1,), (1,)), ((), ()))
 TN = (((0,), (0,)), ((), ()))
 
@@ -162,10 +168,12 @@
 
 
 def step_kernel(
-    patches, key_bias, wqkv, wout, attn_gain, merge_gain, fc1, fc1_bias, fc2, fc2_bias,
-    dest, pick, llm_gain, text_hbm, hidden_hbm,
-    seq_out, layer_out,
-    text, incoming, xn, att, attr, wout_all, f2p, dall, ball, nrm, turn, blk1, rows_all, fc1_all,
+    counts, patches, attn_gain, merge_gain, fc1_bias, fc2_bias, dest_rows, llm_gain,
+    wqkv_hbm, wout_hbm, fc1_hbm, fc2_hbm, text_hbm, hidden_hbm,
+    seq_hbm, layer_hbm,
+    wqkv, wout, fc1, fc2, dest, bias1,
+    text, incoming, stage, seq_out, layer_out,
+    xn, att, attr, wout_all, f2p, dall, ball, nrm, turn, blk1, rows_all, fc1_all,
     blk2, hid_all, fc2_all, acc, second, emb, flat, send_rows, got, sq_own, sq_all,
     send, recv, send3, recv3, local, relay_send, relay_recv,
 ):
@@ -190,10 +198,30 @@
     for peer in peers:
         pl.semaphore_signal(barrier, inc=1, device_id=peer, device_id_type=MESH)
 
-    own_text = pltpu.make_async_copy(text_hbm, text, local.at[0])
-    own_text.start()
-
-    gain1 = attn_gain[...].astype(F32)
+    loads = [
+        pltpu.make_async_copy(a, b, local.at[k])
+        for k, (a, b) in enumerate(
+            ((wout_hbm, wout), (fc2_hbm, fc2), (wqkv_hbm, wqkv), (fc1_hbm, fc1), (text_hbm, text))
+        )
+    ]
+    for copy in loads:
+        copy.start()
+
+    j_lane = lax.broadcasted_iota(jnp.int32, (1, 128), 1)
+    dest_row = dest_rows[...].reshape(1, 128)
+    tile_count = jnp.where(j_lane < 64, counts[0], counts[1])
+    live = (j_lane % 64) * 4 < tile_count
+    dest[...] = jnp.broadcast_to(jnp.where(live, dest_row, 2**30), (8, 128))
+    slot = (dest_row // 512) * 2 + j_lane % 2
+    pick = (lax.broadcasted_iota(jnp.int32, (128, 128), 0) == slot).astype(F32).astype(BF)
+    bias_row = fc1_bias[...].reshape(1, 80)
+    top = lax.broadcasted_iota(jnp.int32, (8, 80), 0) == 0
+    bias_row = jnp.where(top, bias_row.astype(F32), 0.0).astype(BF)
+    bias1[...] = dot(bias_row, jnp.ones((8, 128), BF), TN).astype(BF)
+    k_lane = lax.broadcasted_iota(jnp.int32, (1, 256), 1)
+    key_bias = [jnp.where(k_lane < counts[t], 0.0, -1e30) for t in range(2)]
+
+    gain1 = attn_gain[...].reshape(1, 1280).astype(F32)
 
     def norm_rows(i, carry):
         r = pl.ds(pl.multiple_of(i * 32, 32), 32)
@@ -204,12 +232,56 @@
     pl.semaphore_wait(barrier, len(peers))
 
     cp = Copies(send, recv)
+    relay_to = [at(x, y, zl, 1, m), at(x, (y + 1) % 4, 1, 0, m), at(x, y, 1 - zl, 0, m)]
+    relays = [
+        pltpu.make_async_remote_copy(
+            src_ref=hidden_hbm, dst_ref=ref, send_sem=relay_send.at[k], recv_sem=relay_recv.at[k],
+            device_id=relay_to[k], device_id_type=MESH,
+        )
+        for k, ref in ((0, incoming), (1, stage))
+    ]
+    even_out, odd_out = (c == 1) & (zl == 0), (c == 0) & (zl == 1) & (y > 0)
+    drips = []
+    for k in range(16):
+        r = slice(32 * k, 32 * (k + 1))
+        drips.append(
+            [
+                pltpu.make_async_remote_copy(
+                    src_ref=ref.at[r], dst_ref=incoming.at[r],
+                    send_sem=relay_send.at[2 + k], recv_sem=relay_recv.at[2 + k],
+                    device_id=relay_to[2], device_id_type=MESH,
+                )
+                for ref in (hidden_hbm, stage)
+            ]
+        )
+
+    def drip(k):
+        for j in (2 * k, 2 * k + 1):
+
+            @pl.when(even_out)
+            def _():
+                drips[j][0].start()
+
+            @pl.when(odd_out)
+            def _():
+                drips[j][1].start()
+
+    loads[0].wait()
     half_rows = pl.ds(pl.multiple_of((zl * 2 + c) * 80, 16), 80)
     hop0, finish0 = column_gather(
-        cp, lambda k: (slice(None), slice(640 * k, 640 * (k + 1))), wout.at[half_rows], wout_all, pos
+        cp, BY_ROWS, wout.at[half_rows], wout_all, pos
     )
     hop0(0)
-    wout_all[z, c] = wout[half_rows, :]
+
+    @pl.when((c == 1) & (zl == 1) & (y < 3))
+    def _():
+        relays[1].start()
+
+    @pl.when(c == 0)
+    def _():
+        relays[0].start()
+
+    loads[1].wait()
     pieces, notes, biases = [], [], []
     for dy in range(4):
         for dx in range(4):
@@ -224,17 +296,18 @@
         for dc in range(2):
             if dz or dc:
                 biases.append(
-                    cp.go(fc1_bias, ball.at[zl * 2 + c], at(x, y, (zl + dz) % 2, (c + dc) % 2, m))
+                    cp.go(bias1, ball.at[zl * 2 + c], at(x, y, (zl + dz) % 2, (c + dc) % 2, m))
                 )
     f2p[mine] = fc2[:, pl.ds(pl.multiple_of(mine * 128, 128), 128)]
     dall[pl.ds(pl.multiple_of((s * 4 + x) * 8, 8), 8), :] = dest[...]
-    ball[zl * 2 + c] = fc1_bias[...]
+    ball[zl * 2 + c] = bias1[...]
+    wout_all[z, c] = wout[half_rows, :]
+    loads[2].wait()
 
     lane = lax.broadcasted_iota(jnp.int32, (256, 320), 1)
     for t in range(2):
         xt = xn[256 * t : 256 * (t + 1), :]
         q, k, v = (dot(xt, wqkv[j], NT).astype(BF) for j in range(3))
-        hop0(2 * t + 1)
         out = jnp.zeros((256, 320), F32)
         for h in range(4):
             inside = (lane >= 80 * h) & (lane < 80 * (h + 1))
@@ -243,11 +316,15 @@
             sc = jnp.exp(sc - jnp.max(sc, axis=1, keepdims=True))
             w = (sc / jnp.sum(sc, axis=1, keepdims=True)).astype(BF)
             out = jnp.where(inside, dot(w, v), out)
-            if h == 1:
-                hop0(2 * t + 2)
+            if t == 1 and h == 1:
+                hop0(2)
+        if t == 0:
+            hop0(1)
         att[2 * t : 2 * t + 2] = out.astype(BF).reshape(2, 128, 320)
     parts = [cp.go(att.at[peer[2]], attr.at[m], peer) for peer in across]
     attr[m] = att[m]
+    hop0(3)
+    hop0(4)
     finish0()
     for copy in parts:
         copy.wait_recv()
@@ -255,7 +332,7 @@
         w = wout_all[2 * k : 2 * k + 2].reshape(320, 1280)
         part = dot(attr[k], w)
         nrm[...] = part if k == 0 else nrm[...] + part
-    gain2 = merge_gain[...].astype(F32)
+    gain2 = merge_gain[...].reshape(1, 1280).astype(F32)
     for i in range(4):
         r = pl.ds(pl.multiple_of(m * 128 + 32 * i, 32), 32)
         o = (patches[r, :].astype(F32) + nrm[32 * i : 32 * (i + 1), :]).astype(BF)
@@ -267,11 +344,15 @@
             cols = slice(128 * b, 128 * (b + 1))
             blk1[p, :, cols] = turn[b, pl.ds(p, 32, stride=4), :].astype(BF)
 
-    hop1, finish1 = column_gather(
-        cp, lambda k: (slice(None), slice(640 * k, 640 * (k + 1))), fc1, fc1_all, pos
-    )
+    loads[3].wait()
+
+    @pl.when(odd_out)
+    def _():
+        relays[1].wait_recv()
+
+    hop1, finish1 = column_gather(cp, BY_ROWS, fc1, fc1_all, pos)
     fc1_all[z, c] = fc1[...]
-    plane_gather(cp, blk1, rows_all, hop1, pos)
+    plane_gather(cp, blk1, rows_all, hop1, drip, 0, pos)
     finish1()
     for copy in biases:
         copy.wait_recv()
@@ -286,21 +367,10 @@
 
     for copy in pieces:
         copy.wait_recv()
-    hop2, finish2 = column_gather(
-        cp, lambda k: (slice(8 * k, 8 * (k + 1)),), f2p, fc2_all, pos
-    )
+    hop2, finish2 = column_gather(cp, (slice(0, 8), slice(8, 16)), f2p, fc2_all, pos)
     fc2_all[z, c] = f2p[...]
-    plane_gather(cp, blk2, hid_all, hop2, pos)
+    plane_gather(cp, blk2, hid_all, hop2, drip, 4, pos)
     finish2()
-
-    onward = pltpu.make_async_remote_copy(
-        src_ref=hidden_hbm, dst_ref=incoming, send_sem=relay_send, recv_sem=relay_recv,
-        device_id=((s + 1) % 16, x, m), device_id_type=MESH,
-    )
-
-    @pl.when(s < 15)
-    def _():
-        onward.start()
 
     for b in range(4):
         zl_, c_ = b // 2, b % 2
@@ -325,10 +395,10 @@
     emb[home] = second[m, rows(x, y)]
     for copy in moved:
         copy.wait_recv()
-    bias2 = fc2_bias[...].astype(F32)
+    bias2 = fc2_bias[...].reshape(1, 2048).astype(F32)
     for b in range(16):
         e = (emb[:, 128 * b : 128 * (b + 1)].astype(F32) + bias2[:, 128 * b : 128 * (b + 1)]).astype(BF)
-        flat[pl.ds(b, 128, stride=16), :] = dot(pick[...], e)
+        flat[pl.ds(b, 128, stride=16), :] = dot(pick, e)
     send_rows[...] = flat[...].astype(BF).reshape(64, 32, 128)
     moved = [
         cp3.go(send_rows.at[peer[0] * 4 + peer[1]], got.at[s * 4 + x], peer) for peer in groups
@@ -345,15 +415,16 @@
     for i in range(2):
         spot = jnp.max(jnp.where(here & (odd == i), (d - low).astype(F32), -1.0), axis=1, keepdims=True)
         puts.append((row == spot.astype(jnp.int32)).astype(F32).astype(BF))
-    own_text.wait()
-
-    @pl.when(s < 15)
-    def _():
-        onward.wait_send()
-
-    @pl.when(s > 0)
-    def _():
-        onward.wait_recv()
+    loads[4].wait()
+
+    @pl.when(c == 1)
+    def _():
+        relays[0].wait_recv()
+
+    @pl.when((c == 0) & (s > 0))
+    def _():
+        for k in range(16):
+            drips[k][0].wait_recv()
 
     for copy in moved:
         copy.wait_recv()
@@ -376,6 +447,8 @@
             seq_out[rr, cols] = seq.astype(BF)
             enter = jnp.where(first, seq, incoming[rr, cols].astype(F32))
             squares[r] = squares[r] + enter * enter
+    seq_save = pltpu.make_async_copy(seq_out, seq_hbm, local.at[0])
+    seq_save.start()
     sub = lax.broadcasted_iota(jnp.int32, (8, 128), 0)
     total = jnp.zeros((8, 128), F32)
     for r in range(4):
@@ -388,7 +461,8 @@
         copy.wait_recv()
     total = (sq_all[0] + sq_all[1]) + (sq_all[2] + sq_all[3])
     scale = lax.rsqrt(total / HID + llm_eps)
-    gain3 = llm_gain[...].astype(F32)
+    gain3 = llm_gain[...].reshape(1, 2048).astype(F32)
+    saves = []
     for r in range(4):
         by = jnp.broadcast_to(scale[r : r + 1, :], (128, 128)).T
         rr = slice(128 * r, 128 * (r + 1))
@@ -396,32 +470,52 @@
             cols = slice(128 * b, 128 * (b + 1))
             enter = jnp.where(first, seq_out[rr, cols].astype(F32), incoming[rr, cols].astype(F32))
             layer_out[rr, cols] = (enter * by * gain3[:, cols]).astype(BF)
+        saves.append(pltpu.make_async_copy(layer_out.at[rr], layer_hbm.at[rr], local.at[1 + r]))
+        saves[-1].start()
     cp.drain()
     cp3.drain()
+
+    @pl.when(c == 0)
+    def _():
+        relays[0].wait_send()
+
+    @pl.when((c == 1) & (zl == 1) & (y < 3))
+    def _():
+        relays[1].wait_send()
+
+    @pl.when(even_out | odd_out)
+    def _():
+        for k in range(16):
+            drips[k][0].wait_send()
+
+    seq_save.wait()
+    for copy in saves:
+        copy.wait()
 
 
 def per_device(
     patches, patch_counts, dest_rows, qkv_weight, out_weight, attn_gain, merge_gain,
     fc1_weight, fc1_bias, fc2_weight, fc2_bias, text_embeds, section_hidden, llm_gain,
 ):
-    merged, seq_rows = 128, text_embeds.shape[0]
-    slot_in_tile = jnp.arange(merged, dtype=jnp.int32) % 64
-    live = slot_in_tile * 4 < jnp.repeat(patch_counts, 64, total_repeat_length=merged)
-    dest_live = jnp.broadcast_to(jnp.where(live, dest_rows, 2**30)[None, :], (8, merged))
-    key_live = jnp.arange(256, dtype=jnp.int32)[None, None, :] < patch_counts[:, None, None]
-    key_bias = jnp.where(key_live, 0.0, -1e30).astype(F32)
-    slot = (dest_rows // seq_rows) * 2 + jnp.arange(merged, dtype=jnp.int32) % 2
-    pick = (jnp.arange(merged, dtype=jnp.int32)[:, None] == slot[None, :]).astype(BF)
     vm = pl.BlockSpec(memory_space=pltpu.VMEM)
     hbm = pl.BlockSpec(memory_space=pl.ANY)
     dma = pltpu.SemaphoreType.DMA
-    first_copies = 16 + 15 + 63 + 3 + 3 + 56 + 56
+    first_copies = 23 + 15 + 63 + 3 + 3 + 63 + 63
     return pl.pallas_call(
         step_kernel,
         out_shape=[jax.ShapeDtypeStruct((512, 2048), BF)] * 2,
-        in_specs=[vm] * 13 + [hbm] * 2,
-        out_specs=[vm] * 2,
+        in_specs=[pl.BlockSpec(memory_space=pltpu.SMEM)] + [vm] * 7 + [hbm] * 6,
+        out_specs=[hbm] * 2,
         scratch_shapes=[
+            pltpu.VMEM((3, 320, 1280), BF),
+            pltpu.VMEM((320, 1280), BF),
+            pltpu.VMEM((80, 1280), BF),
+            pltpu.VMEM((80, 2048), BF),
+            pltpu.VMEM((8, 128), jnp.int32),
+            pltpu.VMEM((80, 128), BF),
+            pltpu.VMEM((512, 2048), BF),
+            pltpu.VMEM((512, 2048), BF),
+            pltpu.VMEM((512, 2048), BF),
             pltpu.VMEM((512, 2048), BF),
             pltpu.VMEM((512, 2048), BF),
             pltpu.VMEM((512, 1280), BF),
@@ -451,29 +545,17 @@
             dma((first_copies,)),
             dma((63 + 63 + 3,)),
             dma((63 + 63 + 3,)),
-            dma((1,)),
-            dma,
-            dma,
+            dma((5,)),
+            dma((18,)),
+            dma((18,)),
         ],
         compiler_params=pltpu.CompilerParams(
             collective_id=1, has_side_effects=True, vmem_limit_bytes=60 * 2**20
         ),
     )(
-        patches,
-        key_bias,
-        qkv_weight.transpose(1, 2, 0),
-        out_weight,
-        attn_gain[None, :],
-        merge_gain[None, :],
-        fc1_weight.T,
-        jnp.broadcast_to(fc1_bias[:, None], (80, 128)),
-        fc2_weight,
-        fc2_bias[None, :],
-        dest_live,
-        pick,
-        llm_gain[None, :],
-        text_embeds,
-        section_hidden,
+        patch_counts, patches, attn_gain, merge_gain, fc1_bias, fc2_bias, dest_rows, llm_gain,
+        qkv_weight.transpose(1, 2, 0), out_weight, fc1_weight.T, fc2_weight,
+        text_embeds, section_hidden,
     )
 
 

time: 201 us -> 162 us (0.81)
  Pallas kernels: 182 us -> 155 us
  local copies, waits for them, and re-layouts: 13 us -> 4.63 us
  other arithmetic: 3.89 us -> 0 us
    pallas_call x1, Pallas kernels: 182 us -> 155 us  [per_device(): pl.pallas_call(step_kernel, out_shape=[jax.ShapeDtypeStruct((512, 2048),...]
    broadcast_in_dim x6 -> x0, local copies, waits for them, and re-layouts: 7.06 us -> none  [the longest x1 1.34 us: per_device(): jnp.broadcast_to(fc1_bias[:, None], (80, 128))]
where the time goes in v3:
time: 162 us; the launch traced here: 161 us
  Pallas kernels  155 us (96%)
  local copies, waits for them, and re-layouts  4.63 us (3%)
    pallas_call x1, Pallas kernels, per_device(): pl.pallas_call(step_kernel, out_shape=[jax.ShapeDtypeStruct((512, 2048),...  155 us
    unnamed x4, local copies, waits for them, and re-layouts  4.63 us

profile of v3, /device:TPU:8, one launch (start us, length us, event | category | flops | bytes accessed | tf_op | source)
XLA Modules:
  0.0 160.7 jit_solution(6354582811534587196)
XLA Ops:
  0.6 155.4 %shard_map.149 = (bf16[512,2048]{1,0:T(8,128)(2,1)}, bf16[512,2048]{1,0:T(8,128)(2,1)}) custom-call(s32[2]{0:T(128)} %counts.1, bf16[512,1280]{1,0:T(8,128)(2,1)} %patches.1, bf16[1280]{0:T(1024)(128)(2,1)} %attn_gain.1, bf16[1280]{0:T(1024)(128)(2,1)} %merge_gain.1, bf16[80]{0:T(256)(128)(2,1)} %fc1_bias.1, bf16[2048]{0:T(1024)(128)(2,1)} %fc2_bias.1, ...), custom_call_target="tpu_custom_call" | custom-call | tf_op jit(solution)/shard_map/pallas_call | solution.py:504
  156.1 0.0 copy-start
  156.1 3.3 %copy.18 = bf16[512,2048]{1,0:T(8,128)(2,1)} copy(bf16[512,2048]{1,0:T(8,128)(2,1)} %get-tuple-element.4) | data formatting | bytes 4194304
  159.4 0.0 copy-done
  159.4 1.3 copy.19
Async XLA Ops:
  156.1 3.3 %copy-start = (bf16[512,2048]{1,0:T(8,128)(2,1)S(1)}, bf16[512,2048]{1,0:T(8,128)(2,1)}, u32[]{:S(2)}) copy-start(bf16[512,2048]{1,0:T(8,128)(2,1)} %get-tuple-element.5) | copy-start | bytes 6291460

commit v4 on v3

--- a/solution.py
+++ b/solution.py
@@ -26,37 +26,45 @@
     return (y * 4 + zl * 2 + c, x, m)
 
 
-def greet(peers):
-    barrier = pltpu.get_barrier_semaphore()
-    for peer in peers:
-        pl.semaphore_signal(barrier, inc=1, device_id=peer, device_id_type=MESH)
-    pl.semaphore_wait(barrier, len(peers))
-
-
-class Copies:
+class Wire:
     def __init__(self, send, recv):
-        self.send, self.recv, self.all = send, recv, []
+        self.send, self.recv, self.sends, self.recvs = send, recv, 0, 0
+
+    def batch(self, sent, shared=None):
+        k = self.sends
+        self.sends += 1
+        if shared is not None:
+            shared, self.recvs = self.recvs, self.recvs + 1
+        return Batch(self, k, sent, shared)
+
+
+class Batch:
+    def __init__(self, wire, k, sent, shared):
+        self.wire, self.sem, self.sent, self.shared = wire, wire.send.at[k], sent, shared
+
+    def describe(self, src, dst, k, peer):
+        return pltpu.make_async_remote_copy(
+            src_ref=src, dst_ref=dst, send_sem=self.sem, recv_sem=self.wire.recv.at[k],
+            device_id=peer, device_id_type=MESH,
+        )
 
     def go(self, src, dst, peer):
-        k = len(self.all)
-        copy = pltpu.make_async_remote_copy(
-            src_ref=src,
-            dst_ref=dst,
-            send_sem=self.send.at[k],
-            recv_sem=self.recv.at[k],
-            device_id=peer,
-            device_id_type=MESH,
-        )
+        k = self.shared
+        if k is None:
+            k, self.wire.recvs = self.wire.recvs, self.wire.recvs + 1
+        copy = self.describe(src, dst, k, peer)
         copy.start()
-        self.all.append(copy)
+        self.peer = peer
         return copy
 
-    def drain(self):
-        for copy in self.all:
-            copy.wait_send()
-
-
-def column_gather(cp, halves, col, column, pos):
+    def wait_recv(self):
+        self.describe(self.sent, self.sent, self.shared, self.peer).wait_recv()
+
+    def wait_send(self):
+        self.describe(self.sent, self.sent, 0, self.peer).wait_send()
+
+
+def column_gather(wire, ring_bytes, side_bytes, halves, col, column, pos, upward=(0,)):
     x, y, zl, c, m = pos
     z = 2 * m + zl
     zs = [(z + k) % 8 for k in range(8)]
@@ -65,35 +73,77 @@
         return at(x, y, zz % 2, cc, zz // 2)
 
     above, below, twin = zdev(zs[1], c), zdev(zs[7], c), zdev(z, 1 - c)
-    up, down, side = {}, {}, []
+    up, down = {}, {}
+    up_far, down_far = upward, tuple(j for j in range(2) if j not in upward)
+    ring, side = wire.batch(ring_bytes), wire.batch(side_bytes, shared=True)
 
     def hop(k):
         if k == 0:
             for j in range(2):
                 src, dst = col.at[halves[j]], column.at[z, c].at[halves[j]]
-                up[1, j] = cp.go(src, dst, above)
-                down[1, j] = cp.go(src, dst, below)
-            side.append(cp.go(col, column.at[z, c], twin))
+                up[1, j] = ring.go(src, dst, above)
+                down[1, j] = ring.go(src, dst, below)
+            side.go(col, column.at[z, c], twin)
             return
         for j in range(2):
-            for ways, z_from, peer, last in ((up, zs[8 - k], above, 0), (down, zs[k % 8], below, 1)):
-                if k < 4 or j == last:
+            for ways, z_from, peer, far in ((up, zs[8 - k], above, up_far), (down, zs[k], below, down_far)):
+                if k < 4 or j in far:
                     ways[k, j].wait_recv()
-                if k < 3 or (k == 3 and j == last):
+                if k < 3 or (k == 3 and j in far):
                     ref = column.at[z_from, c].at[halves[j]]
-                    ways[k + 1, j] = cp.go(ref, ref, peer)
+                    ways[k + 1, j] = ring.go(ref, ref, peer)
         for z_from in [zs[8 - k], zs[k]][: 2 if k < 4 else 1]:
             ref = column.at[z_from, c]
-            side.append(cp.go(ref, ref, twin))
+            side.go(ref, ref, twin)
+
+    return hop, side.wait_recv, [ring, side]
+
+
+def shared_gather(wire, col, column, half_bytes, side_bytes, pos):
+    x, y, zl, c, m = pos
+    z = 2 * m + zl
+    zs = [(z + k) % 8 for k in range(8)]
+
+    def zdev(zz, cc):
+        return at(x, y, zz % 2, cc, zz // 2)
+
+    above, below, twin = zdev(zs[1], c), zdev(zs[7], c), zdev(z, 1 - c)
+    right, left = at((x + 1) % 4, y, zl, c, m), at((x + 3) % 4, y, zl, c, m)
+    mine = pl.ds(pl.multiple_of((x % 2) * 640, 128), 640)
+    other = pl.ds(pl.multiple_of((1 - x % 2) * 640, 128), 640)
+    ring, across = wire.batch(half_bytes), wire.batch(half_bytes)
+    side = wire.batch(side_bytes, shared=True)
+    ways = {}
+    crossed = []
+
+    def hop(k):
+        if k == 0:
+            dst = column.at[z, c].at[:, mine]
+            ways["up", 1] = ring.go(col.at[:, mine], dst, above)
+            ways["down", 1] = ring.go(col.at[:, mine], dst, below)
+            side.go(col, column.at[z, c], twin)
+            return
+        for way, z_from, peer, beside, end in (
+            ("up", zs[8 - k], above, right, 4), ("down", zs[k], below, left, 3)
+        ):
+            if k <= end:
+                ways[way, k].wait_recv()
+                ref = column.at[z_from, c].at[:, mine]
+                if k < end:
+                    ways[way, k + 1] = ring.go(ref, ref, peer)
+                crossed.append((across.go(ref, ref, beside), column.at[z_from, c].at[:, other]))
+                side.go(ref, ref, twin)
 
     def finish():
-        for copy in side:
+        for copy, ref in crossed:
             copy.wait_recv()
-
-    return hop, finish
-
-
-def plane_gather(cp, blk, plane, hop, drip, first, pos):
+            side.go(ref, ref, twin)
+        side.wait_recv()
+
+    return hop, finish, [ring, across, side]
+
+
+def plane_gather(cp, blk, plane, points, pos):
     x, y, zl, c, m = pos
     xs = [(x + k) % 4 for k in range(4)]
     ys = [(y + k) % 4 for k in range(4)]
@@ -116,7 +166,7 @@
     for v in range(2):
         for g in (1, -1):
             three[v, 0, g] = push(v, 1, g, 0, 0, own=True)
-    hop(0)
+    points[0]()
     plane[:, y, x] = blk[...]
     for g in (1, -1):
         for v in range(2):
@@ -125,8 +175,7 @@
             two[v, g] = push(v, 0, g, a, 0, *((0, 1) if g > 0 else (1, 2)))
             for h in (1, -1):
                 three[v, a, h] = push(v, 1, h, a, 0)
-    hop(1)
-    drip(first + 0)
+    points[1]()
 
     def opposite(a):
         for g in (1, -1):
@@ -140,15 +189,12 @@
             two[v, g].wait_recv()
         for h in (1, -1):
             three[v, 2, h] = push(v, 1, h, 2, 0)
-    hop(2)
-    drip(first + 1)
+    points[2]()
     opposite(3)
     opposite(1)
-    hop(3)
-    drip(first + 2)
+    points[3]()
     opposite(2)
-    hop(4)
-    drip(first + 3)
+    points[4]()
     for copy in four.values():
         copy.wait_recv()
 
@@ -170,12 +216,12 @@
 def step_kernel(
     counts, patches, attn_gain, merge_gain, fc1_bias, fc2_bias, dest_rows, llm_gain,
     wqkv_hbm, wout_hbm, fc1_hbm, fc2_hbm, text_hbm, hidden_hbm,
-    seq_hbm, layer_hbm,
+    seq_out, layer_out,
     wqkv, wout, fc1, fc2, dest, bias1,
-    text, incoming, stage, seq_out, layer_out,
+    text, incoming, stage,
     xn, att, attr, wout_all, f2p, dall, ball, nrm, turn, blk1, rows_all, fc1_all,
     blk2, hid_all, fc2_all, acc, second, emb, flat, send_rows, got, sq_own, sq_all,
-    send, recv, send3, recv3, local, relay_send, relay_recv,
+    send, recv, local, relay_send, relay_recv,
 ):
     pos = place()
     x, y, zl, c, m = pos
@@ -207,31 +253,9 @@
     for copy in loads:
         copy.start()
 
-    j_lane = lax.broadcasted_iota(jnp.int32, (1, 128), 1)
-    dest_row = dest_rows[...].reshape(1, 128)
-    tile_count = jnp.where(j_lane < 64, counts[0], counts[1])
-    live = (j_lane % 64) * 4 < tile_count
-    dest[...] = jnp.broadcast_to(jnp.where(live, dest_row, 2**30), (8, 128))
-    slot = (dest_row // 512) * 2 + j_lane % 2
-    pick = (lax.broadcasted_iota(jnp.int32, (128, 128), 0) == slot).astype(F32).astype(BF)
-    bias_row = fc1_bias[...].reshape(1, 80)
-    top = lax.broadcasted_iota(jnp.int32, (8, 80), 0) == 0
-    bias_row = jnp.where(top, bias_row.astype(F32), 0.0).astype(BF)
-    bias1[...] = dot(bias_row, jnp.ones((8, 128), BF), TN).astype(BF)
-    k_lane = lax.broadcasted_iota(jnp.int32, (1, 256), 1)
-    key_bias = [jnp.where(k_lane < counts[t], 0.0, -1e30) for t in range(2)]
-
-    gain1 = attn_gain[...].reshape(1, 1280).astype(F32)
-
-    def norm_rows(i, carry):
-        r = pl.ds(pl.multiple_of(i * 32, 32), 32)
-        xn[r, :] = normed(patches[r, :].astype(F32), gain1).astype(BF)
-        return carry
-
-    lax.fori_loop(0, 16, norm_rows, 0)
     pl.semaphore_wait(barrier, len(peers))
 
-    cp = Copies(send, recv)
+    wire = Wire(send, recv)
     relay_to = [at(x, y, zl, 1, m), at(x, (y + 1) % 4, 1, 0, m), at(x, y, 1 - zl, 0, m)]
     relays = [
         pltpu.make_async_remote_copy(
@@ -248,15 +272,19 @@
             [
                 pltpu.make_async_remote_copy(
                     src_ref=ref.at[r], dst_ref=incoming.at[r],
-                    send_sem=relay_send.at[2 + k], recv_sem=relay_recv.at[2 + k],
+                    send_sem=relay_send.at[2], recv_sem=relay_recv.at[2],
                     device_id=relay_to[2], device_id_type=MESH,
                 )
                 for ref in (hidden_hbm, stage)
             ]
         )
+    all_drips = pltpu.make_async_remote_copy(
+        src_ref=stage, dst_ref=incoming, send_sem=relay_send.at[2], recv_sem=relay_recv.at[2],
+        device_id=relay_to[2], device_id_type=MESH,
+    )
 
     def drip(k):
-        for j in (2 * k, 2 * k + 1):
+        for j in range((0, 2, 4, 6, 7, 9, 11, 12, 12)[k], (2, 4, 6, 7, 9, 11, 12, 12, 16)[k]):
 
             @pl.when(even_out)
             def _():
@@ -268,8 +296,8 @@
 
     loads[0].wait()
     half_rows = pl.ds(pl.multiple_of((zl * 2 + c) * 80, 16), 80)
-    hop0, finish0 = column_gather(
-        cp, BY_ROWS, wout.at[half_rows], wout_all, pos
+    hop0, finish0, batches = shared_gather(
+        wire, wout.at[half_rows], wout_all, fc1_all.at[0:7, 0, :, 0:640], fc1_all.at[0:4], pos
     )
     hop0(0)
 
@@ -282,28 +310,53 @@
         relays[0].start()
 
     loads[1].wait()
-    pieces, notes, biases = [], [], []
+    pieces = wire.batch(f2p.at[0:15], shared=True)
+    notes = wire.batch(dall.at[0:63], shared=True)
+    biases = wire.batch(ball.at[0:3], shared=True)
+    parts = wire.batch(attr.at[0:3], shared=True)
+    batches += [pieces, notes, biases, parts]
     for dy in range(4):
         for dx in range(4):
             if dx or dy:
                 px, py = (x + dx) % 4, (y + dy) % 4
                 cols = pl.ds(pl.multiple_of((py * 4 + px) * 128, 128), 128)
-                pieces.append(cp.go(fc2.at[:, cols], f2p.at[mine], at(px, py, zl, c, m)))
+                pieces.go(fc2.at[:, cols], f2p.at[mine], at(px, py, zl, c, m))
+    j_lane = lax.broadcasted_iota(jnp.int32, (1, 128), 1)
+    dest_row = dest_rows[...].reshape(1, 128)
+    tile_count = jnp.where(j_lane < 64, counts[0], counts[1])
+    live = (j_lane % 64) * 4 < tile_count
+    dest[...] = jnp.where(live, dest_row, 2**30)
+    slot = (dest_row // 512) * 2 + j_lane % 2
+    pick = (lax.broadcasted_iota(jnp.int32, (128, 128), 0) == slot).astype(F32).astype(BF)
+    bias_row = fc1_bias[...].reshape(1, 80)
+    top = lax.broadcasted_iota(jnp.int32, (8, 80), 0) == 0
+    bias_row = jnp.where(top, bias_row.astype(F32), 0.0).astype(BF)
+    bias1[...] = dot(bias_row, jnp.ones((8, 128), BF), TN).astype(BF)
+    k_lane = lax.broadcasted_iota(jnp.int32, (1, 256), 1)
+    key_bias = [jnp.where(k_lane < counts[t], 0.0, -1e30) for t in range(2)]
+
     for peer in groups:
-        spot = dall.at[pl.ds(pl.multiple_of((s * 4 + x) * 8, 8), 8)]
-        notes.append(cp.go(dest, spot, peer))
+        notes.go(dest, dall.at[s * 4 + x], peer)
     for dz in range(2):
         for dc in range(2):
             if dz or dc:
-                biases.append(
-                    cp.go(bias1, ball.at[zl * 2 + c], at(x, y, (zl + dz) % 2, (c + dc) % 2, m))
-                )
+                biases.go(bias1, ball.at[zl * 2 + c], at(x, y, (zl + dz) % 2, (c + dc) % 2, m))
     f2p[mine] = fc2[:, pl.ds(pl.multiple_of(mine * 128, 128), 128)]
-    dall[pl.ds(pl.multiple_of((s * 4 + x) * 8, 8), 8), :] = dest[...]
+    dall[s * 4 + x] = dest[...]
     ball[zl * 2 + c] = bias1[...]
     wout_all[z, c] = wout[half_rows, :]
     loads[2].wait()
 
+    gain1 = attn_gain[...].reshape(1, 1280).astype(F32)
+
+    def norm_rows(i, carry):
+        r = pl.ds(pl.multiple_of(i * 32, 32), 32)
+        xn[r, :] = normed(patches[r, :].astype(F32), gain1).astype(BF)
+        return carry
+
+    lax.fori_loop(0, 16, norm_rows, 0)
+
+    hop0(1)
     lane = lax.broadcasted_iota(jnp.int32, (256, 320), 1)
     for t in range(2):
         xt = xn[256 * t : 256 * (t + 1), :]
@@ -316,18 +369,14 @@
             sc = jnp.exp(sc - jnp.max(sc, axis=1, keepdims=True))
             w = (sc / jnp.sum(sc, axis=1, keepdims=True)).astype(BF)
             out = jnp.where(inside, dot(w, v), out)
-            if t == 1 and h == 1:
-                hop0(2)
-        if t == 0:
-            hop0(1)
         att[2 * t : 2 * t + 2] = out.astype(BF).reshape(2, 128, 320)
-    parts = [cp.go(att.at[peer[2]], attr.at[m], peer) for peer in across]
+    for peer in across:
+        parts.go(att.at[peer[2]], attr.at[m], peer)
     attr[m] = att[m]
-    hop0(3)
-    hop0(4)
+    for k in range(2, 5):
+        hop0(k)
     finish0()
-    for copy in parts:
-        copy.wait_recv()
+    parts.wait_recv()
     for k in range(4):
         w = wout_all[2 * k : 2 * k + 2].reshape(320, 1280)
         part = dot(attr[k], w)
@@ -350,12 +399,41 @@
     def _():
         relays[1].wait_recv()
 
-    hop1, finish1 = column_gather(cp, BY_ROWS, fc1, fc1_all, pos)
+    hop1, finish1, more = column_gather(
+        wire, fc1_all.at[0:7, 0], fc1_all.at[0:4], BY_ROWS, fc1, fc1_all, pos
+    )
+    planes = [wire.batch(fc2_all.at[:, :, 0:15]) for _ in range(2)]
+    batches += more + planes
     fc1_all[z, c] = fc1[...]
-    plane_gather(cp, blk1, rows_all, hop1, drip, 0, pos)
+
+    def point(*calls):
+        def run():
+            for call, k in calls:
+                call(k)
+
+        return run
+
+    pieces.wait_recv()
+    hop2, finish2, more = column_gather(
+        wire, fc2_all.at[0:7, 0], fc2_all.at[0:4], (slice(0, 8), slice(8, 16)), f2p, fc2_all, pos
+    )
+    batches += more
+    fc2_all[z, c] = f2p[...]
+    plane_gather(
+        planes[0],
+        blk1,
+        rows_all,
+        [
+            point((hop1, 0)),
+            point((hop1, 1), (drip, 0)),
+            point((hop1, 2), (drip, 1)),
+            point((hop1, 3), (drip, 2)),
+            point((hop1, 4), (hop2, 0), (drip, 3)),
+        ],
+        pos,
+    )
     finish1()
-    for copy in biases:
-        copy.wait_recv()
+    biases.wait_recv()
     for p in range(4):
         part = dot(
             fc1_all[2 * p : 2 * p + 2].reshape(320, 1280), rows_all[p].reshape(512, 1280), NT
@@ -365,11 +443,19 @@
         h = acc[80 * b : 80 * (b + 1), :] + ball[b][:, :1].astype(F32)
         blk2[b] = (0.5 * h * (1.0 + lax.erf(h * 0.5**0.5))).astype(BF)
 
-    for copy in pieces:
-        copy.wait_recv()
-    hop2, finish2 = column_gather(cp, (slice(0, 8), slice(8, 16)), f2p, fc2_all, pos)
-    fc2_all[z, c] = f2p[...]
-    plane_gather(cp, blk2, hid_all, hop2, drip, 4, pos)
+    plane_gather(
+        planes[1],
+        blk2,
+        hid_all,
+        [
+            point(),
+            point((hop2, 1), (drip, 4)),
+            point((hop2, 2), (drip, 5)),
+            point((hop2, 3), (drip, 6)),
+            point((hop2, 4), (drip, 7)),
+        ],
+        pos,
+    )
     finish2()
 
     for b in range(4):
@@ -382,31 +468,30 @@
     for k in range(4):
         second[k] = acc[:, 128 * k : 128 * (k + 1)].astype(BF)
 
-    cp3 = Copies(send3, recv3)
+    homes = wire.batch(got.at[0:63], shared=True)
+    picked = wire.batch(got.at[0:63], shared=True)
+    sums = wire.batch(sq_all.at[0:3], shared=True)
+    batches += [homes, picked, sums]
 
     def rows(px, py):
         return pl.ds(pl.multiple_of((py * 4 + px) * 32, 32), 32)
 
     home = (pl.ds(pl.multiple_of(m * 32, 32), 32), pl.ds(pl.multiple_of(mine * 128, 128), 128))
-    moved = [
-        cp3.go(second.at[pm, rows(px, py)], emb.at[home], at(px, py, zl, c, pm))
-        for px, py, pm in owners
-    ]
+    for px, py, pm in owners:
+        homes.go(second.at[pm, rows(px, py)], emb.at[home], at(px, py, zl, c, pm))
     emb[home] = second[m, rows(x, y)]
-    for copy in moved:
-        copy.wait_recv()
+    homes.wait_recv()
     bias2 = fc2_bias[...].reshape(1, 2048).astype(F32)
     for b in range(16):
         e = (emb[:, 128 * b : 128 * (b + 1)].astype(F32) + bias2[:, 128 * b : 128 * (b + 1)]).astype(BF)
         flat[pl.ds(b, 128, stride=16), :] = dot(pick, e)
     send_rows[...] = flat[...].astype(BF).reshape(64, 32, 128)
-    moved = [
-        cp3.go(send_rows.at[peer[0] * 4 + peer[1]], got.at[s * 4 + x], peer) for peer in groups
-    ]
+    for peer in groups:
+        picked.go(send_rows.at[peer[0] * 4 + peer[1]], got.at[s * 4 + x], peer)
+    drip(8)
     got[s * 4 + x] = send_rows[s * 4 + x]
-    for copy in notes:
-        copy.wait_recv()
-    d = dall[pl.ds(0, 64, stride=8), :]
+    notes.wait_recv()
+    d = dall[...].reshape(64, 128)
     low = (s * 4 + x) * 512
     row = lax.broadcasted_iota(jnp.int32, (64, 512), 1)
     odd = lax.broadcasted_iota(jnp.int32, (64, 128), 1) % 2
@@ -423,11 +508,9 @@
 
     @pl.when((c == 0) & (s > 0))
     def _():
-        for k in range(16):
-            drips[k][0].wait_recv()
-
-    for copy in moved:
-        copy.wait_recv()
+        all_drips.wait_recv()
+
+    picked.wait_recv()
     flat[...] = got[...].reshape(2048, 128).astype(F32)
     ones = jnp.ones((64, 128), BF)
     first = s == 0
@@ -447,22 +530,19 @@
             seq_out[rr, cols] = seq.astype(BF)
             enter = jnp.where(first, seq, incoming[rr, cols].astype(F32))
             squares[r] = squares[r] + enter * enter
-    seq_save = pltpu.make_async_copy(seq_out, seq_hbm, local.at[0])
-    seq_save.start()
     sub = lax.broadcasted_iota(jnp.int32, (8, 128), 0)
     total = jnp.zeros((8, 128), F32)
     for r in range(4):
         line = jnp.broadcast_to(jnp.sum(squares[r], axis=1, keepdims=True), (128, 128)).T
         total = jnp.where(sub == r, line[0:8], total)
     sq_own[...] = total
-    moved = [cp3.go(sq_own, sq_all.at[m], peer) for peer in across]
+    for peer in across:
+        sums.go(sq_own, sq_all.at[m], peer)
     sq_all[m] = total
-    for copy in moved:
-        copy.wait_recv()
+    sums.wait_recv()
     total = (sq_all[0] + sq_all[1]) + (sq_all[2] + sq_all[3])
     scale = lax.rsqrt(total / HID + llm_eps)
     gain3 = llm_gain[...].reshape(1, 2048).astype(F32)
-    saves = []
     for r in range(4):
         by = jnp.broadcast_to(scale[r : r + 1, :], (128, 128)).T
         rr = slice(128 * r, 128 * (r + 1))
@@ -470,10 +550,8 @@
             cols = slice(128 * b, 128 * (b + 1))
             enter = jnp.where(first, seq_out[rr, cols].astype(F32), incoming[rr, cols].astype(F32))
             layer_out[rr, cols] = (enter * by * gain3[:, cols]).astype(BF)
-        saves.append(pltpu.make_async_copy(layer_out.at[rr], layer_hbm.at[rr], local.at[1 + r]))
-        saves[-1].start()
-    cp.drain()
-    cp3.drain()
+    for batch in batches:
+        batch.wait_send()
 
     @pl.when(c == 0)
     def _():
@@ -485,12 +563,7 @@
 
     @pl.when(even_out | odd_out)
     def _():
-        for k in range(16):
-            drips[k][0].wait_send()
-
-    seq_save.wait()
-    for copy in saves:
-        copy.wait()
+        all_drips.wait_send()
 
 
 def per_device(
@@ -500,21 +573,18 @@
     vm = pl.BlockSpec(memory_space=pltpu.VMEM)
     hbm = pl.BlockSpec(memory_space=pl.ANY)
     dma = pltpu.SemaphoreType.DMA
-    first_copies = 23 + 15 + 63 + 3 + 3 + 63 + 63
     return pl.pallas_call(
         step_kernel,
-        out_shape=[jax.ShapeDtypeStruct((512, 2048), BF)] * 2,
+        out_shape=[pltpu.VMEM((512, 2048), BF)] * 2,
         in_specs=[pl.BlockSpec(memory_space=pltpu.SMEM)] + [vm] * 7 + [hbm] * 6,
-        out_specs=[hbm] * 2,
+        out_specs=[vm] * 2,
         scratch_shapes=[
             pltpu.VMEM((3, 320, 1280), BF),
             pltpu.VMEM((320, 1280), BF),
             pltpu.VMEM((80, 1280), BF),
             pltpu.VMEM((80, 2048), BF),
-            pltpu.VMEM((8, 128), jnp.int32),
+            pltpu.VMEM((1, 128), jnp.int32),
             pltpu.VMEM((80, 128), BF),
-            pltpu.VMEM((512, 2048), BF),
-            pltpu.VMEM((512, 2048), BF),
             pltpu.VMEM((512, 2048), BF),
             pltpu.VMEM((512, 2048), BF),
             pltpu.VMEM((512, 2048), BF),
@@ -523,7 +593,7 @@
             pltpu.VMEM((4, 128, 320), BF),
             pltpu.VMEM((8, 2, 80, 1280), BF),
             pltpu.VMEM((16, 80, 128), BF),
-            pltpu.VMEM((512, 128), jnp.int32),
+            pltpu.VMEM((64, 1, 128), jnp.int32),
             pltpu.VMEM((4, 80, 128), BF),
             pltpu.VMEM((128, 1280), F32),
             pltpu.VMEM((10, 128, 128), F32),
@@ -541,16 +611,14 @@
             pltpu.VMEM((64, 32, 128), BF),
             pltpu.VMEM((8, 128), F32),
             pltpu.VMEM((4, 8, 128), F32),
-            dma((first_copies,)),
-            dma((first_copies,)),
-            dma((63 + 63 + 3,)),
-            dma((63 + 63 + 3,)),
+            dma((16,)),
+            dma((3 * 15 + 80 + 7,)),
             dma((5,)),
-            dma((18,)),
-            dma((18,)),
+            dma((3,)),
+            dma((3,)),
         ],
         compiler_params=pltpu.CompilerParams(
-            collective_id=1, has_side_effects=True, vmem_limit_bytes=60 * 2**20
+            collective_id=1, has_side_effects=True, vmem_limit_bytes=54 * 2**20
         ),
     )(
         patch_counts, patches, attn_gain, merge_gain, fc1_bias, fc2_bias, dest_rows, llm_gain,

time: 162 us -> 155 us (0.957)
  Pallas kernels: 155 us -> 152 us
  local copies, waits for them, and re-layouts: 4.63 us -> 2.64 us
    pallas_call x1, Pallas kernels: 155 us -> 152 us  [per_device(): pl.pallas_call(step_kernel, out_shape=[pltpu.VMEM((512, 2048), BF)] * 2,...]
    unnamed x4 -> x2, local copies, waits for them, and re-layouts: 4.63 us -> 2.64 us
where the time goes in v4:
time: 155 us
  Pallas kernels  152 us (98%)
  local copies, waits for them, and re-layouts  2.64 us (2%)
    pallas_call x1, Pallas kernels, per_device(): pl.pallas_call(step_kernel, out_shape=[pltpu.VMEM((512, 2048), BF)] * 2,...  152 us

profile of v4, /device:TPU:8, one launch (start us, length us, event | category | flops | bytes accessed | tf_op | source)
XLA Modules:
  0.0 155.3 jit_solution(12770497578538310794)
XLA Ops:
  0.6 152.0 %shard_map.149 = (bf16[512,2048]{1,0:T(8,128)(2,1)S(1)}, bf16[512,2048]{1,0:T(8,128)(2,1)S(1)}) custom-call(s32[2]{0:T(128)} %counts.1, bf16[512,1280]{1,0:T(8,128)(2,1)} %patches.1, bf16[1280]{0:T(1024)(128)(2,1)} %attn_gain.1, bf16[1280]{0:T(1024)(128)(2,1)} %merge_gain.1, bf16[80]{0:T(256)(128)(2,1)} %fc1_bias.1, bf16[2048]{0:T(1024)(128)(2,1)} %fc2_bias.1, ...), custom_call_target="tpu_custom_call" | custom-call | tf_op jit(solution)/shard_map/pallas_call | solution.py:576
  152.7 1.3 copy.18
  154.0 1.3 copy.19

commit v5 on v4

--- a/solution.py
+++ b/solution.py
@@ -220,7 +220,7 @@
     wqkv, wout, fc1, fc2, dest, bias1,
     text, incoming, stage,
     xn, att, attr, wout_all, f2p, dall, ball, nrm, turn, blk1, rows_all, fc1_all,
-    blk2, hid_all, fc2_all, acc, second, emb, flat, send_rows, got, sq_own, sq_all,
+    blk2, hid_all, fc2_all, acc1, acc, second, mid, emb, flat, send_rows, got, sq_own, sq_all,
     send, recv, local, relay_send, relay_recv,
 ):
     pos = place()
@@ -228,19 +228,12 @@
     s = y * 4 + zl * 2 + c
     z = 2 * m + zl
     mine = y * 4 + x
+    note = (zl * 2 + c) * 16 + mine
     across = [(s, x, (m + k) % 4) for k in (2, 1, 3)]
     groups = [((s + i) % 16, (x + j) % 4, m) for i in range(16) for j in range(4) if i or j]
-    owners = [
-        ((x + i) % 4, (y + j) % 4, (m + k) % 4)
-        for i in range(4) for j in range(4) for k in range(4) if i or j or k
-    ]
     barrier = pltpu.get_barrier_semaphore()
-    cross = [
-        at((x + i) % 4, (y + j) % 4, zl, c, (m + k) % 4)
-        for i in range(4) for j in range(4) for k in range(1, 4) if i or j
-    ]
     column = [at(x, y, 1 - zl, c, (m + 1) % 4), at(x, y, 1 - zl, c, (m + 3) % 4)]
-    peers = across + groups + cross + column
+    peers = across + groups + column
     for peer in peers:
         pl.semaphore_signal(barrier, inc=1, device_id=peer, device_id_type=MESH)
 
@@ -284,7 +277,7 @@
     )
 
     def drip(k):
-        for j in range((0, 2, 4, 6, 7, 9, 11, 12, 12)[k], (2, 4, 6, 7, 9, 11, 12, 12, 16)[k]):
+        for j in range((0, 3, 6, 9, 11, 13, 15, 16, 16)[k], (3, 6, 9, 11, 13, 15, 16, 16, 16)[k]):
 
             @pl.when(even_out)
             def _():
@@ -326,8 +319,6 @@
     tile_count = jnp.where(j_lane < 64, counts[0], counts[1])
     live = (j_lane % 64) * 4 < tile_count
     dest[...] = jnp.where(live, dest_row, 2**30)
-    slot = (dest_row // 512) * 2 + j_lane % 2
-    pick = (lax.broadcasted_iota(jnp.int32, (128, 128), 0) == slot).astype(F32).astype(BF)
     bias_row = fc1_bias[...].reshape(1, 80)
     top = lax.broadcasted_iota(jnp.int32, (8, 80), 0) == 0
     bias_row = jnp.where(top, bias_row.astype(F32), 0.0).astype(BF)
@@ -336,13 +327,13 @@
     key_bias = [jnp.where(k_lane < counts[t], 0.0, -1e30) for t in range(2)]
 
     for peer in groups:
-        notes.go(dest, dall.at[s * 4 + x], peer)
+        notes.go(dest, dall.at[note], peer)
     for dz in range(2):
         for dc in range(2):
             if dz or dc:
                 biases.go(bias1, ball.at[zl * 2 + c], at(x, y, (zl + dz) % 2, (c + dc) % 2, m))
     f2p[mine] = fc2[:, pl.ds(pl.multiple_of(mine * 128, 128), 128)]
-    dall[s * 4 + x] = dest[...]
+    dall[note] = dest[...]
     ball[zl * 2 + c] = bias1[...]
     wout_all[z, c] = wout[half_rows, :]
     loads[2].wait()
@@ -370,10 +361,11 @@
             w = (sc / jnp.sum(sc, axis=1, keepdims=True)).astype(BF)
             out = jnp.where(inside, dot(w, v), out)
         att[2 * t : 2 * t + 2] = out.astype(BF).reshape(2, 128, 320)
+    hop0(2)
     for peer in across:
         parts.go(att.at[peer[2]], attr.at[m], peer)
     attr[m] = att[m]
-    for k in range(2, 5):
+    for k in range(3, 5):
         hop0(k)
     finish0()
     parts.wait_recv()
@@ -438,9 +430,9 @@
         part = dot(
             fc1_all[2 * p : 2 * p + 2].reshape(320, 1280), rows_all[p].reshape(512, 1280), NT
         )
-        acc[0:320, :] = part if p == 0 else acc[0:320, :] + part
+        acc1[...] = part if p == 0 else acc1[...] + part
     for b in range(4):
-        h = acc[80 * b : 80 * (b + 1), :] + ball[b][:, :1].astype(F32)
+        h = acc1[80 * b : 80 * (b + 1), :] + ball[b][:, :1].astype(F32)
         blk2[b] = (0.5 * h * (1.0 + lax.erf(h * 0.5**0.5))).astype(BF)
 
     plane_gather(
@@ -458,43 +450,58 @@
     )
     finish2()
 
-    for b in range(4):
-        zl_, c_ = b // 2, b % 2
-        w = jnp.concatenate(
-            [fc2_all[2 * k + zl_, c_].reshape(1280, 128) for k in range(4)], axis=1
-        )
-        part = dot(hid_all[b].reshape(1280, 512), w, TN)
-        acc[...] = part if b == 0 else acc[...] + part
-    for k in range(4):
-        second[k] = acc[:, 128 * k : 128 * (k + 1)].astype(BF)
-
-    homes = wire.batch(got.at[0:63], shared=True)
+    direct = wire.batch(emb.at[0:2], shared=True)
+    halfway = wire.batch(emb.at[0])
+    onward = wire.batch(emb.at[0], shared=True)
     picked = wire.batch(got.at[0:63], shared=True)
     sums = wire.batch(sq_all.at[0:3], shared=True)
-    batches += [homes, picked, sums]
-
-    def rows(px, py):
-        return pl.ds(pl.multiple_of((py * 4 + px) * 32, 32), 32)
-
-    home = (pl.ds(pl.multiple_of(m * 32, 32), 32), pl.ds(pl.multiple_of(mine * 128, 128), 128))
-    for px, py, pm in owners:
-        homes.go(second.at[pm, rows(px, py)], emb.at[home], at(px, py, zl, c, pm))
-    emb[home] = second[m, rows(x, y)]
-    homes.wait_recv()
+    batches += [direct, halfway, onward, picked, sums]
+    ms = [(m + k) % 4 for k in range(4)]
+    upper, lower = slice(0, 256), slice(256, 512)
+    via = []
+    for half in range(2):
+        r = (upper, lower)[half]
+        for b in range(4):
+            w = jnp.concatenate(
+                [fc2_all[2 * k + b // 2, b % 2].reshape(1280, 128) for k in range(4)], axis=1
+            )
+            part = dot(hid_all[b, :, :, :, r].reshape(1280, 256), w, TN)
+            acc[...] = part if b == 0 else acc[...] + part
+        for k in range(4):
+            second[k, r, :] = acc[:, 128 * k : 128 * (k + 1)].astype(BF)
+        via.append(halfway.go(second.at[ms[2], r], mid.at[half], across[1 + half]))
+        for k in (1, 3):
+            direct.go(second.at[ms[k], r], emb.at[m, r], across[1 + k // 2])
+    emb[m] = second[m]
+    for half in range(2):
+        via[half].wait_recv()
+        r = (upper, lower)[half]
+        onward.go(mid.at[half], emb.at[ms[3 - 2 * half], r], across[1 + half])
+    notes.wait_recv()
+    near = dall[pl.ds(pl.multiple_of((zl * 2 + c) * 16, 16), 16)]
+    receiver = lax.broadcasted_iota(jnp.int32, (64, 128), 0)
+    odd = lax.broadcasted_iota(jnp.int32, (64, 128), 1) % 2
     bias2 = fc2_bias[...].reshape(1, 2048).astype(F32)
+    own_bias = jnp.zeros((1, 128), F32)
     for b in range(16):
-        e = (emb[:, 128 * b : 128 * (b + 1)].astype(F32) + bias2[:, 128 * b : 128 * (b + 1)]).astype(BF)
-        flat[pl.ds(b, 128, stride=16), :] = dot(pick, e)
+        own_bias = jnp.where(mine == b, bias2[:, 128 * b : 128 * (b + 1)], own_bias)
+    direct.wait_recv()
+    onward.wait_recv()
+    for q in range(16):
+        e = emb[:, 32 * q : 32 * (q + 1), :].reshape(128, 128)
+        e = (e.astype(F32) + own_bias).astype(BF)
+        to_here = receiver == near[q] // 512
+        for i in range(2):
+            pick = (to_here & (odd == i)).astype(F32).astype(BF)
+            flat[pl.ds(2 * q + i, 64, stride=32), :] = dot(pick, e)
     send_rows[...] = flat[...].astype(BF).reshape(64, 32, 128)
     for peer in groups:
         picked.go(send_rows.at[peer[0] * 4 + peer[1]], got.at[s * 4 + x], peer)
     drip(8)
     got[s * 4 + x] = send_rows[s * 4 + x]
-    notes.wait_recv()
     d = dall[...].reshape(64, 128)
     low = (s * 4 + x) * 512
     row = lax.broadcasted_iota(jnp.int32, (64, 512), 1)
-    odd = lax.broadcasted_iota(jnp.int32, (64, 128), 1) % 2
     here = (d >= low) & (d < low + 512)
     puts = []
     for i in range(2):
@@ -521,7 +528,16 @@
         for r in range(4)
     ]
     for b in range(16):
-        new = [flat[pl.ds(16 * i + b, 64, stride=32), :].astype(BF) for i in range(2)]
+        new = [
+            jnp.concatenate(
+                [
+                    flat[pl.ds(((b // 4 * 4 + zc) * 4 + b % 4) * 32 + i, 16, stride=2), :]
+                    for zc in range(4)
+                ],
+                axis=0,
+            ).astype(BF)
+            for i in range(2)
+        ]
         cols = slice(128 * b, 128 * (b + 1))
         for r in range(4):
             rr = slice(128 * r, 128 * (r + 1))
@@ -603,16 +619,18 @@
             pltpu.VMEM((4, 80, 512), BF),
             pltpu.VMEM((4, 4, 4, 80, 512), BF),
             pltpu.VMEM((8, 2, 16, 80, 128), BF),
-            pltpu.VMEM((512, 512), F32),
+            pltpu.VMEM((320, 512), F32),
+            pltpu.VMEM((256, 512), F32),
             pltpu.VMEM((4, 512, 128), BF),
-            pltpu.VMEM((128, 2048), BF),
+            pltpu.VMEM((2, 256, 128), BF),
+            pltpu.VMEM((4, 512, 128), BF),
             pltpu.VMEM((2048, 128), F32),
             pltpu.VMEM((64, 32, 128), BF),
             pltpu.VMEM((64, 32, 128), BF),
             pltpu.VMEM((8, 128), F32),
             pltpu.VMEM((4, 8, 128), F32),
-            dma((16,)),
-            dma((3 * 15 + 80 + 7,)),
+            dma((18,)),
+            dma((3 * 15 + 80 + 10,)),
             dma((5,)),
             dma((3,)),
             dma((3,)),

time: 155 us -> 147 us (0.948)
  Pallas kernels: 152 us -> 143 us
    pallas_call x1, Pallas kernels: 152 us -> 143 us  [per_device(): pl.pallas_call(step_kernel, out_shape=[pltpu.VMEM((512, 2048), BF)] * 2,...]
where the time goes in v5:
time: 147 us; the launch traced here: 146 us
  Pallas kernels  143 us (97%)
  local copies, waits for them, and re-layouts  2.64 us (2%)
    pallas_call x1, Pallas kernels, per_device(): pl.pallas_call(step_kernel, out_shape=[pltpu.VMEM((512, 2048), BF)] * 2,...  143 us

profile of v5, /device:TPU:8, one launch (start us, length us, event | category | flops | bytes accessed | tf_op | source)
XLA Modules:
  0.0 146.2 jit_solution(17403203221782917782)
XLA Ops:
  0.6 143.0 %shard_map.149 = (bf16[512,2048]{1,0:T(8,128)(2,1)S(1)}, bf16[512,2048]{1,0:T(8,128)(2,1)S(1)}) custom-call(s32[2]{0:T(128)} %counts.1, bf16[512,1280]{1,0:T(8,128)(2,1)} %patches.1, bf16[1280]{0:T(1024)(128)(2,1)} %attn_gain.1, bf16[1280]{0:T(1024)(128)(2,1)} %merge_gain.1, bf16[80]{0:T(256)(128)(2,1)} %fc1_bias.1, bf16[2048]{0:T(1024)(128)(2,1)} %fc2_bias.1, ...), custom_call_target="tpu_custom_call" | custom-call | tf_op jit(solution)/shard_map/pallas_call | solution.py:592
  143.6 1.3 copy.18
  144.9 1.3 copy.19

commit v6 on v5

--- a/solution.py
+++ b/solution.py
@@ -177,24 +177,26 @@
                 three[v, a, h] = push(v, 1, h, a, 0)
     points[1]()
 
-    def opposite(a):
+    def opposite(a, between=None):
         for g in (1, -1):
             for v in range(2):
                 three[v, a, g].wait_recv()
                 four[v, a, g] = push(v, 1, g, a, -g % 4, *((0, 1) if g > 0 else (1, 2)))
-
-    opposite(0)
+            if between is not None and g == 1:
+                between()
+
+    opposite(0, points[2])
     for v in range(2):
         for g in (1, -1):
             two[v, g].wait_recv()
         for h in (1, -1):
             three[v, 2, h] = push(v, 1, h, 2, 0)
-    points[2]()
+    points[3]()
     opposite(3)
     opposite(1)
-    points[3]()
+    points[4]()
     opposite(2)
-    points[4]()
+    points[5]()
     for copy in four.values():
         copy.wait_recv()
 
@@ -219,7 +221,7 @@
     seq_out, layer_out,
     wqkv, wout, fc1, fc2, dest, bias1,
     text, incoming, stage,
-    xn, att, attr, wout_all, f2p, dall, ball, nrm, turn, blk1, rows_all, fc1_all,
+    xn, att, att_mid, attr, wout_all, f2p, dall, ball, nrm, turn, blk1, rows_all, fc1_all,
     blk2, hid_all, fc2_all, acc1, acc, second, mid, emb, flat, send_rows, got, sq_own, sq_all,
     send, recv, local, relay_send, relay_recv,
 ):
@@ -252,32 +254,56 @@
     relay_to = [at(x, y, zl, 1, m), at(x, (y + 1) % 4, 1, 0, m), at(x, y, 1 - zl, 0, m)]
     relays = [
         pltpu.make_async_remote_copy(
-            src_ref=hidden_hbm, dst_ref=ref, send_sem=relay_send.at[k], recv_sem=relay_recv.at[k],
+            src_ref=src, dst_ref=ref, send_sem=relay_send.at[k], recv_sem=relay_recv.at[k],
             device_id=relay_to[k], device_id_type=MESH,
         )
-        for k, ref in ((0, incoming), (1, stage))
+        for k, src, ref in ((0, hidden_hbm, incoming), (1, hidden_hbm.at[256:512], stage))
     ]
+    early_out = (c == 1) & (s < 15)
+    earlies = [
+        pltpu.make_async_remote_copy(
+            src_ref=hidden_hbm.at[32 * k : 32 * (k + 1)],
+            dst_ref=incoming.at[32 * k : 32 * (k + 1)],
+            send_sem=relay_send.at[3], recv_sem=relay_recv.at[2],
+            device_id=((s + 1) % 16, x, m), device_id_type=MESH,
+        )
+        for k in range(8)
+    ]
+
+    def early(lo, hi):
+        @pl.when(early_out)
+        def _():
+            for k in range(lo, hi):
+                earlies[k].start()
+
     even_out, odd_out = (c == 1) & (zl == 0), (c == 0) & (zl == 1) & (y > 0)
     drips = []
-    for k in range(16):
-        r = slice(32 * k, 32 * (k + 1))
+    for k in range(8):
+        r, r_stage = (slice(32 * k + low, 32 * (k + 1) + low) for low in (256, 0))
         drips.append(
             [
                 pltpu.make_async_remote_copy(
-                    src_ref=ref.at[r], dst_ref=incoming.at[r],
+                    src_ref=ref, dst_ref=incoming.at[r],
                     send_sem=relay_send.at[2], recv_sem=relay_recv.at[2],
                     device_id=relay_to[2], device_id_type=MESH,
                 )
-                for ref in (hidden_hbm, stage)
+                for ref in (hidden_hbm.at[r], stage.at[r_stage])
             ]
         )
-    all_drips = pltpu.make_async_remote_copy(
-        src_ref=stage, dst_ref=incoming, send_sem=relay_send.at[2], recv_sem=relay_recv.at[2],
+    all_in = pltpu.make_async_remote_copy(
+        src_ref=incoming, dst_ref=incoming, send_sem=relay_send.at[2], recv_sem=relay_recv.at[2],
         device_id=relay_to[2], device_id_type=MESH,
     )
+    drips_out, earlies_out = (
+        pltpu.make_async_remote_copy(
+            src_ref=stage, dst_ref=stage, send_sem=relay_send.at[k], recv_sem=relay_recv.at[2],
+            device_id=relay_to[2], device_id_type=MESH,
+        )
+        for k in (2, 3)
+    )
 
     def drip(k):
-        for j in range((0, 3, 6, 9, 11, 13, 15, 16, 16)[k], (3, 6, 9, 11, 13, 15, 16, 16, 16)[k]):
+        for j in range((0, 2, 4, 5, 6, 7, 8, 8)[k], (2, 4, 5, 6, 7, 8, 8, 8)[k]):
 
             @pl.when(even_out)
             def _():
@@ -302,12 +328,15 @@
     def _():
         relays[0].start()
 
+    early(0, 3)
+
     loads[1].wait()
     pieces = wire.batch(f2p.at[0:15], shared=True)
     notes = wire.batch(dall.at[0:63], shared=True)
     biases = wire.batch(ball.at[0:3], shared=True)
-    parts = wire.batch(attr.at[0:3], shared=True)
-    batches += [pieces, notes, biases, parts]
+    parts = wire.batch(attr.at[0:2], shared=True)
+    parts_by, parts_on = wire.batch(attr.at[0]), wire.batch(attr.at[0], shared=True)
+    batches += [pieces, notes, biases, parts, parts_by, parts_on]
     for dy in range(4):
         for dx in range(4):
             if dx or dy:
@@ -348,6 +377,7 @@
     lax.fori_loop(0, 16, norm_rows, 0)
 
     hop0(1)
+    early(3, 5)
     lane = lax.broadcasted_iota(jnp.int32, (256, 320), 1)
     for t in range(2):
         xt = xn[256 * t : 256 * (t + 1), :]
@@ -362,13 +392,24 @@
             out = jnp.where(inside, dot(w, v), out)
         att[2 * t : 2 * t + 2] = out.astype(BF).reshape(2, 128, 320)
     hop0(2)
-    for peer in across:
-        parts.go(att.at[peer[2]], attr.at[m], peer)
+    ms = [(m + k) % 4 for k in range(4)]
+    halves = (slice(0, 64), slice(64, 128))
+    via = [
+        parts_by.go(att.at[ms[2], halves[k]], att_mid.at[k], across[1 + k]) for k in range(2)
+    ]
+    parts.go(att.at[ms[1]], attr.at[m], across[1])
+    parts.go(att.at[ms[3]], attr.at[m], across[2])
     attr[m] = att[m]
-    for k in range(3, 5):
-        hop0(k)
+    hop0(3)
+    early(5, 6)
+    for k in range(2):
+        via[k].wait_recv()
+        parts_on.go(att_mid.at[k], attr.at[ms[3 - 2 * k], halves[k]], across[1 + k])
+    hop0(4)
+    early(6, 8)
     finish0()
     parts.wait_recv()
+    parts_on.wait_recv()
     for k in range(4):
         w = wout_all[2 * k : 2 * k + 2].reshape(320, 1280)
         part = dot(attr[k], w)
@@ -421,6 +462,7 @@
             point((hop1, 2), (drip, 1)),
             point((hop1, 3), (drip, 2)),
             point((hop1, 4), (hop2, 0), (drip, 3)),
+            point(),
         ],
         pos,
     )
@@ -445,6 +487,7 @@
             point((hop2, 2), (drip, 5)),
             point((hop2, 3), (drip, 6)),
             point((hop2, 4), (drip, 7)),
+            point(),
         ],
         pos,
     )
@@ -497,7 +540,6 @@
     send_rows[...] = flat[...].astype(BF).reshape(64, 32, 128)
     for peer in groups:
         picked.go(send_rows.at[peer[0] * 4 + peer[1]], got.at[s * 4 + x], peer)
-    drip(8)
     got[s * 4 + x] = send_rows[s * 4 + x]
     d = dall[...].reshape(64, 128)
     low = (s * 4 + x) * 512
@@ -515,7 +557,7 @@
 
     @pl.when((c == 0) & (s > 0))
     def _():
-        all_drips.wait_recv()
+        all_in.wait_recv()
 
     picked.wait_recv()
     flat[...] = got[...].reshape(2048, 128).astype(F32)
@@ -579,7 +621,11 @@
 
     @pl.when(even_out | odd_out)
     def _():
-        all_drips.wait_send()
+        drips_out.wait_send()
+
+    @pl.when(early_out)
+    def _():
+        earlies_out.wait_send()
 
 
 def per_device(
@@ -603,9 +649,10 @@
             pltpu.VMEM((80, 128), BF),
             pltpu.VMEM((512, 2048), BF),
             pltpu.VMEM((512, 2048), BF),
-            pltpu.VMEM((512, 2048), BF),
+            pltpu.VMEM((256, 2048), BF),
             pltpu.VMEM((512, 1280), BF),
             pltpu.VMEM((4, 128, 320), BF),
+            pltpu.VMEM((2, 64, 320), BF),
             pltpu.VMEM((4, 128, 320), BF),
             pltpu.VMEM((8, 2, 80, 1280), BF),
             pltpu.VMEM((16, 80, 128), BF),
@@ -629,10 +676,10 @@
             pltpu.VMEM((64, 32, 128), BF),
             pltpu.VMEM((8, 128), F32),
             pltpu.VMEM((4, 8, 128), F32),
-            dma((18,)),
-            dma((3 * 15 + 80 + 10,)),
+            dma((20,)),
+            dma((3 * 15 + 80 + 13,)),
             dma((5,)),
-            dma((3,)),
+            dma((4,)),
             dma((3,)),
         ],
         compiler_params=pltpu.CompilerParams(

time: 147 us -> 140 us (0.952)
  Pallas kernels: 143 us -> 136 us
    pallas_call x1, Pallas kernels: 143 us -> 136 us  [per_device(): pl.pallas_call(step_kernel, out_shape=[pltpu.VMEM((512, 2048), BF)] * 2,...]
where the time goes in v6:
time: 140 us; the launch traced here: 139 us
  Pallas kernels  136 us (97%)
  local copies, waits for them, and re-layouts  2.64 us (2%)
    pallas_call x1, Pallas kernels, per_device(): pl.pallas_call(step_kernel, out_shape=[pltpu.VMEM((512, 2048), BF)] * 2,...  136 us

profile of v6, /device:TPU:8, one launch (start us, length us, event | category | flops | bytes accessed | tf_op | source)
XLA Modules:
  0.0 139.4 jit_solution(6275533790035541966)
XLA Ops:
  0.6 136.1 %shard_map.149 = (bf16[512,2048]{1,0:T(8,128)(2,1)S(1)}, bf16[512,2048]{1,0:T(8,128)(2,1)S(1)}) custom-call(s32[2]{0:T(128)} %counts.1, bf16[512,1280]{1,0:T(8,128)(2,1)} %patches.1, bf16[1280]{0:T(1024)(128)(2,1)} %attn_gain.1, bf16[1280]{0:T(1024)(128)(2,1)} %merge_gain.1, bf16[80]{0:T(256)(128)(2,1)} %fc1_bias.1, bf16[2048]{0:T(1024)(128)(2,1)} %fc2_bias.1, ...), custom_call_target="tpu_custom_call" | custom-call | tf_op jit(solution)/shard_map/pallas_call | solution.py:638
  136.8 1.3 copy.18
  138.1 1.3 copy.19

commit v7 on v6

--- a/solution.py
+++ b/solution.py
@@ -257,7 +257,7 @@
             src_ref=src, dst_ref=ref, send_sem=relay_send.at[k], recv_sem=relay_recv.at[k],
             device_id=relay_to[k], device_id_type=MESH,
         )
-        for k, src, ref in ((0, hidden_hbm, incoming), (1, hidden_hbm.at[256:512], stage))
+        for k, src, ref in ((0, hidden_hbm, incoming), (1, hidden_hbm.at[192:512], stage))
     ]
     early_out = (c == 1) & (s < 15)
     earlies = [
@@ -267,7 +267,7 @@
             send_sem=relay_send.at[3], recv_sem=relay_recv.at[2],
             device_id=((s + 1) % 16, x, m), device_id_type=MESH,
         )
-        for k in range(8)
+        for k in range(6)
     ]
 
     def early(lo, hi):
@@ -278,8 +278,8 @@
 
     even_out, odd_out = (c == 1) & (zl == 0), (c == 0) & (zl == 1) & (y > 0)
     drips = []
-    for k in range(8):
-        r, r_stage = (slice(32 * k + low, 32 * (k + 1) + low) for low in (256, 0))
+    for k in range(10):
+        r, r_stage = (slice(32 * k + low, 32 * (k + 1) + low) for low in (192, 0))
         drips.append(
             [
                 pltpu.make_async_remote_copy(
@@ -296,14 +296,14 @@
     )
     drips_out, earlies_out = (
         pltpu.make_async_remote_copy(
-            src_ref=stage, dst_ref=stage, send_sem=relay_send.at[k], recv_sem=relay_recv.at[2],
+            src_ref=ref, dst_ref=ref, send_sem=relay_send.at[k], recv_sem=relay_recv.at[2],
             device_id=relay_to[2], device_id_type=MESH,
         )
-        for k in (2, 3)
+        for k, ref in ((2, stage), (3, incoming.at[0:192]))
     )
 
     def drip(k):
-        for j in range((0, 2, 4, 5, 6, 7, 8, 8)[k], (2, 4, 5, 6, 7, 8, 8, 8)[k]):
+        for j in range((0, 2, 4, 6, 7, 8, 9, 10)[k], (2, 4, 6, 7, 8, 9, 10, 10)[k]):
 
             @pl.when(even_out)
             def _():
@@ -406,7 +406,6 @@
         via[k].wait_recv()
         parts_on.go(att_mid.at[k], attr.at[ms[3 - 2 * k], halves[k]], across[1 + k])
     hop0(4)
-    early(6, 8)
     finish0()
     parts.wait_recv()
     parts_on.wait_recv()
@@ -649,7 +648,7 @@
             pltpu.VMEM((80, 128), BF),
             pltpu.VMEM((512, 2048), BF),
             pltpu.VMEM((512, 2048), BF),
-            pltpu.VMEM((256, 2048), BF),
+            pltpu.VMEM((320, 2048), BF),
             pltpu.VMEM((512, 1280), BF),
             pltpu.VMEM((4, 128, 320), BF),
             pltpu.VMEM((2, 64, 320), BF),

time: 140 us -> 141 us (level)
  no operation moved by 1% of the time
where the time goes in v7:
time: 141 us; the launch traced here: 140 us
  Pallas kernels  137 us (97%)
  local copies, waits for them, and re-layouts  2.64 us (2%)
    pallas_call x1, Pallas kernels, per_device(): pl.pallas_call(step_kernel, out_shape=[pltpu.VMEM((512, 2048), BF)] * 2,...  137 us

profile of v7, /device:TPU:8, one launch (start us, length us, event | category | flops | bytes accessed | tf_op | source)
XLA Modules:
  0.0 140.2 jit_solution(8124236243672298080)
XLA Ops:
  0.6 136.9 %shard_map.149 = (bf16[512,2048]{1,0:T(8,128)(2,1)S(1)}, bf16[512,2048]{1,0:T(8,128)(2,1)S(1)}) custom-call(s32[2]{0:T(128)} %counts.1, bf16[512,1280]{1,0:T(8,128)(2,1)} %patches.1, bf16[1280]{0:T(1024)(128)(2,1)} %attn_gain.1, bf16[1280]{0:T(1024)(128)(2,1)} %merge_gain.1, bf16[80]{0:T(256)(128)(2,1)} %fc1_bias.1, bf16[2048]{0:T(1024)(128)(2,1)} %fc2_bias.1, ...), custom_call_target="tpu_custom_call" | custom-call | tf_op jit(solution)/shard_map/pallas_call | solution.py:637
  137.6 1.3 copy.18
  138.9 1.3 copy.19
